TPU v7x, 32 devices: a 4x4x1 block of a 4x4x8 slice. The times are simulated.
32 devices in a mesh: case: 1 (over z), model: 4 (over y), ens: 8 (over x, core).
Axes of the slice: x: 4, y: 4, z: 1, core: 2. Of those that a mesh axis runs over, the one named last changes fastest.
The devices are a block of a 4x4x8 slice.
Arguments:
- ens_init: float32 [32, 5120, 64], P(('case', 'ens'), None, 'model')
- mix_op: bfloat16 [5120, 5120], replicated
- w_in: bfloat16 [3, 64, 1024], P(None, None, 'model')
- w_out: bfloat16 [3, 1024, 64], P(None, 'model')
- obs_val: float32 [2, 5120, 32], P(None, ('case', 'ens', 'model'))
- obs_prec: float32 [5120, 32], P(('case', 'ens', 'model'))
- obs_idx: int32 [32], replicated
- inflation: float32 [1], replicated
Outputs:
- output: float32 [32, 5120, 64], P(('case', 'ens'), None, 'model')
All inputs are finite; a program needn't handle non-finite values.
Results may differ from a plain program's by a relative error of at most 0.0131299.
Values are sent between devices in bfloat16 or wider.
A program may use at most 768 MiB of HBM per device.

v0:
```python
import jax
import jax.numpy as jnp
from jax import lax
from jax.sharding import PartitionSpec as P

NS_STEPS = 12
FULL_PREC = lax.Precision.HIGHEST


def value_a8(ens_state, mix_op, w_in, w_out):
    for layer_idx in range(w_in.shape[0]):
        mix_out = jnp.einsum('ij,jkc->ikc', mix_op, ens_state.astype(jnp.bfloat16), preferred_element_type=jnp.float32).astype(jnp.bfloat16)
        mix_full = lax.all_gather(mix_out, 'model', axis=2, tiled=True)
        hidden = jax.nn.gelu(jnp.einsum('ikv,vf->ikf', mix_full, w_in[layer_idx], preferred_element_type=jnp.float32), approximate=True)
        part_sum = jnp.einsum('ikf,fv->ikv', hidden.astype(jnp.bfloat16), w_out[layer_idx], preferred_element_type=jnp.float32)
        ens_state = ens_state + lax.psum_scatter(part_sum, 'model', scatter_dimension=2, tiled=True)
    return ens_state


def letkf_weights(col_state, obs_now, prec_now, obs_idx, inflation):
    members = col_state.shape[-2]
    ens_mean = jnp.mean(col_state, axis=-2)
    anomaly = col_state - ens_mean[..., None, :]
    obs_anom = jnp.take(anomaly, obs_idx, axis=-1)
    innovation = obs_now - jnp.take(ens_mean, obs_idx, axis=-1)
    weighted = obs_anom * prec_now[..., None, :]
    identity = jnp.eye(members, dtype=jnp.float32)
    a_tilde = ((members - 1) / inflation[0]) * identity + jnp.einsum('...ip,...jp->...ij', weighted, obs_anom, precision=FULL_PREC)
    trace_sum = jnp.trace(a_tilde, axis1=-2, axis2=-1)[..., None, None]
    b_mat = a_tilde / trace_sum
    t_mat = 1.5 * identity - 0.5 * b_mat
    z_mat = t_mat
    for ns_step in range(1, NS_STEPS):
        b_mat = jnp.matmul(b_mat, t_mat, precision=FULL_PREC)
        t_mat = 1.5 * identity - 0.5 * jnp.matmul(z_mat, b_mat, precision=FULL_PREC)
        z_mat = jnp.matmul(t_mat, z_mat, precision=FULL_PREC)
    sqrt_inv = z_mat / jnp.sqrt(trace_sum)
    gain_vec = jnp.einsum('...ip,...p->...i', weighted, innovation, precision=FULL_PREC)
    half_step = jnp.einsum('...ij,...j->...i', sqrt_inv, gain_vec, precision=FULL_PREC)
    w_mean = jnp.einsum('...ij,...j->...i', sqrt_inv, half_step, precision=FULL_PREC)
    w_full = (members - 1) ** 0.5 * sqrt_inv + w_mean[..., None]
    return ens_mean, anomaly, w_full


def solution(mesh):
    def local_step(ens_local, mix_op, w_in, w_out, obs_val, obs_prec, obs_idx, inflation):
        ens_state = jnp.transpose(ens_local, (1, 0, 2))
        for cycle_idx in range(obs_val.shape[0]):
            ens_state = value_a8(ens_state, mix_op, w_in, w_out)
            col_state = lax.all_to_all(ens_state, 'ens', 0, 1, tiled=True)
            col_state = lax.all_to_all(col_state, 'model', 0, 2, tiled=True)
            ens_mean, anomaly, w_full = letkf_weights(col_state, obs_val[cycle_idx], obs_prec, obs_idx, inflation)
            col_state = ens_mean[:, None, :] + jnp.einsum('bik,biv->bkv', w_full, anomaly, precision=FULL_PREC)
            col_state = lax.all_to_all(col_state, 'model', 2, 0, tiled=True)
            ens_state = lax.all_to_all(col_state, 'ens', 1, 0, tiled=True)
        return jnp.transpose(ens_state, (1, 0, 2))

    member_spec = P(('case', 'ens'), None, 'model')
    col_axes = ('case', 'ens', 'model')
    in_specs = (member_spec, P(None, None), P(None, None, 'model'), P(None, 'model', None), P(None, col_axes, None), P(col_axes, None), P(None), P(None))
    return jax.shard_map(local_step, mesh=mesh, in_specs=in_specs, out_specs=member_spec, check_vma=False)
```

profile of v0, /device:TPU:97, one launch (start us, length us, event | category | flops | bytes accessed | tf_op | source)
XLA Modules:
  0.0 1419.0 jit_solution(14270177351878104716)
XLA Ops:
  7.9 24.5 %fusion.388 = f32[5120,64]{0,1:S(1)} fusion(bf16[5120,5120]{1,0:T(8,128)(2,1)} %param.13, bf16[5120,64]{0,1:T(8,128)(2,1)S(1)} %bitcast.328), kind=kOutput, calls=%fused_computation.393 | convolution fusion | flops 3355443200 | bytes 54394880
  33.6 36.1 %all-gather.7.cloned.1.call-done = bf16[5120,4,64]{0,2,1:T(8,128)(2,1)} async-done(((bf16[5120,4,16]{0,2,1:T(8,128)(2,1)}), bf16[5120,4,64]{0,2,1:T(8,128)(2,1)}) %all-gather.7.cloned.1.call-update) | async-done | bytes 2621456 | tf_op jit(solution)/shard_map/all_gather | solution.py:13
  69.6 13.3 fusion.68
  83.5 52.7 %reduce-scatter.7.cloned.1.call-done = f32[5120,4,16]{0,2,1:T(8,128)} async-done(((f32[5120,4,64]{0,2,1:T(8,128)}), f32[5120,4,16]{0,2,1:T(8,128)}) %reduce-scatter.7.cloned.1.call-update) | async-done | bytes 1310736 | tf_op jit(solution)/shard_map/reduce_scatter | solution.py:16
  136.2 22.9 %fusion.97 = bf16[5120,4,16]{0,2,1:T(8,128)(2,1)} fusion(bf16[5120,5120]{1,0:T(8,128)(2,1)} %param.13, f32[5120,4,16]{0,2,1:T(8,128)} %reduce-scatter.7.cloned.1.call-done, f32[4,5120,16]{1,2,0:T(8,128)S(1)} %copy-done.2), kind=kOutput, calls=%fused_computation.83 | convolution fusion | flops 3356426240 | bytes 55705600 | tf_op jit(solution)/shard_map/ij,jkc->ikc/dot_general | solution.py:12
  159.3 32.1 %all-gather.9.cloned.1.call-done = bf16[5120,4,64]{0,2,1:T(8,128)(2,1)} async-done(((bf16[5120,4,16]{0,2,1:T(8,128)(2,1)}), bf16[5120,4,64]{0,2,1:T(8,128)(2,1)}) %all-gather.9.cloned.1.call-update) | async-done | bytes 2621456 | tf_op jit(solution)/shard_map/all_gather | solution.py:13
  191.3 13.2 fusion.66
  204.7 53.2 %reduce-scatter.9.cloned.1.call-done = f32[5120,4,16]{0,2,1:T(8,128)} async-done(((f32[5120,4,64]{0,2,1:T(8,128)}), f32[5120,4,16]{0,2,1:T(8,128)}) %reduce-scatter.9.cloned.1.call-update) | async-done | bytes 1310736 | tf_op jit(solution)/shard_map/reduce_scatter | solution.py:16
  257.9 22.9 %fusion.94 = bf16[5120,4,16]{0,2,1:T(8,128)(2,1)} fusion(bf16[5120,5120]{1,0:T(8,128)(2,1)} %param.13, f32[5120,4,16]{0,2,1:T(8,128)} %reduce-scatter.9.cloned.1.call-done, f32[5120,4,16]{0,2,1:T(8,128)S(1)} %copy-done.3, f32[4,5120,16]{1,2,0:T(8,128)S(1)} %copy-done.2), kind=kOutput, calls=%fused_computation.82 | convolution fusion | flops 3356753920 | bytes 57016320 | tf_op jit(solution)/shard_map/ij,jkc->ikc/dot_general | solution.py:12
  281.0 32.1 %all-gather.11.cloned.1.call-done = bf16[5120,4,64]{0,2,1:T(8,128)(2,1)} async-done(((bf16[5120,4,16]{0,2,1:T(8,128)(2,1)}), bf16[5120,4,64]{0,2,1:T(8,128)(2,1)}) %all-gather.11.cloned.1.call-update) | async-done | bytes 2621456 | tf_op jit(solution)/shard_map/all_gather | solution.py:13
  313.0 13.2 fusion.64
  326.3 53.3 %reduce-scatter.11.cloned.1.call-done = f32[5120,4,16]{0,2,1:T(8,128)} async-done(((f32[5120,4,64]{0,2,1:T(8,128)}), f32[5120,4,16]{0,2,1:T(8,128)}) %reduce-scatter.11.cloned.1.call-update) | async-done | bytes 1310736 | tf_op jit(solution)/shard_map/reduce_scatter | solution.py:16
  401.2 22.9 %all_to_all.144 = f32[8,1,40960]{2,1,0:T(1,128)S(1)} all-to-all(f32[8,1,40960]{2,1,0:T(1,128)S(1)} %reshape.121), channel_id=1, replica_groups=mesh['case'=1,'model'=4,'ens'=8] {'ens'}, dimensions={0} | all-to-all | bytes 2621440 | tf_op jit(solution)/shard_map/all_to_all | solution.py:50
  462.3 15.5 %all-to-all-done.1 = f32[4,1,81920]{2,1,0:T(1,128)S(1)} async-done(((f32[4,1,81920]{2,1,0:T(1,128)}), f32[4,1,81920]{2,1,0:T(1,128)S(1)}, u32[]{:S(2)}, u32[]{:S(2)}) %all-to-all-start.1) | async-done | bytes 1310752 | tf_op jit(solution)/shard_map/all_to_all | solution.py:51
  661.9 26.5 %all_to_all.145 = f32[160,32,64]{0,1,2:T(8,128)S(1)} all-to-all(f32[160,32,64]{0,1,2:T(8,128)S(1)} %copy.168), channel_id=1, replica_groups=mesh['case'=1,'model'=4,'ens'=8] {'model'}, dimensions={2} | all-to-all | bytes 2621440 | tf_op jit(solution)/shard_map/all_to_all | solution.py:54
  691.1 23.6 %all_to_all.146 = f32[640,32,16]{0,2,1:T(8,128)S(1)} all-to-all(f32[640,32,16]{0,2,1:T(8,128)S(1)} %all_to_all.115), channel_id=1, replica_groups=mesh['case'=1,'model'=4,'ens'=8] {'ens'}, dimensions={1} | all-to-all | bytes 2621440 | tf_op jit(solution)/shard_map/all_to_all | solution.py:55
  714.8 22.9 %fusion.91 = bf16[5120,4,16]{0,2,1:T(8,128)(2,1)} fusion(bf16[5120,5120]{1,0:T(8,128)(2,1)} %param.13, f32[5120,4,16]{0,2,1:T(8,128)S(1)} %bitcast.313), kind=kOutput, calls=%fused_computation.81 | convolution fusion | flops 3356098560 | bytes 54394880 | tf_op jit(solution)/shard_map/ij,jkc->ikc/dot_general | solution.py:12
  737.9 30.1 %all-gather.13.cloned.1.call-done = bf16[5120,4,64]{0,2,1:T(8,128)(2,1)} async-done(((bf16[5120,4,16]{0,2,1:T(8,128)(2,1)}), bf16[5120,4,64]{0,2,1:T(8,128)(2,1)}) %all-gather.13.cloned.1.call-update) | async-done | bytes 2621456 | tf_op jit(solution)/shard_map/all_gather | solution.py:13
  768.0 13.2 fusion.62
  781.8 52.8 %reduce-scatter.13.cloned.1.call-done = f32[5120,4,16]{0,2,1:T(8,128)} async-done(((f32[5120,4,64]{0,2,1:T(8,128)}), f32[5120,4,16]{0,2,1:T(8,128)}) %reduce-scatter.13.cloned.1.call-update) | async-done | bytes 1310736 | tf_op jit(solution)/shard_map/reduce_scatter | solution.py:16
  836.0 22.9 %fusion.88 = bf16[5120,4,16]{0,2,1:T(8,128)(2,1)} fusion(bf16[5120,5120]{1,0:T(8,128)(2,1)} %param.13, f32[5120,4,16]{0,2,1:T(8,128)S(1)} %add.141), kind=kOutput, calls=%fused_computation.80 | convolution fusion | flops 3356098560 | bytes 54394880 | tf_op jit(solution)/shard_map/ij,jkc->ikc/dot_general | solution.py:12
  859.1 32.1 %all-gather.15.cloned.1.call-done = bf16[5120,4,64]{0,2,1:T(8,128)(2,1)} async-done(((bf16[5120,4,16]{0,2,1:T(8,128)(2,1)}), bf16[5120,4,64]{0,2,1:T(8,128)(2,1)}) %all-gather.15.cloned.1.call-update) | async-done | bytes 2621456 | tf_op jit(solution)/shard_map/all_gather | solution.py:13
  891.1 13.2 fusion.60
  904.5 53.2 %reduce-scatter.15.cloned.1.call-done = f32[5120,4,16]{0,2,1:T(8,128)} async-done(((f32[5120,4,64]{0,2,1:T(8,128)}), f32[5120,4,16]{0,2,1:T(8,128)}) %reduce-scatter.15.cloned.1.call-update) | async-done | bytes 1310736 | tf_op jit(solution)/shard_map/reduce_scatter | solution.py:16
  959.2 22.9 %fusion.85 = bf16[5120,4,16]{0,2,1:T(8,128)(2,1)} fusion(bf16[5120,5120]{1,0:T(8,128)(2,1)} %param.13, f32[5120,4,16]{0,2,1:T(8,128)S(1)} %add.144), kind=kOutput, calls=%fused_computation.79 | convolution fusion | flops 3356098560 | bytes 54394880 | tf_op jit(solution)/shard_map/ij,jkc->ikc/dot_general | solution.py:12
  982.2 32.1 %all-gather.17.cloned.1.call-done = bf16[5120,4,64]{0,2,1:T(8,128)(2,1)} async-done(((bf16[5120,4,16]{0,2,1:T(8,128)(2,1)}), bf16[5120,4,64]{0,2,1:T(8,128)(2,1)}) %all-gather.17.cloned.1.call-update) | async-done | bytes 2621456 | tf_op jit(solution)/shard_map/all_gather | solution.py:13
  1014.3 13.2 fusion.58
  1027.6 53.3 %reduce-scatter.17.cloned.1.call-done = f32[5120,4,16]{0,2,1:T(8,128)} async-done(((f32[5120,4,64]{0,2,1:T(8,128)}), f32[5120,4,16]{0,2,1:T(8,128)}) %reduce-scatter.17.cloned.1.call-update) | async-done | bytes 1310736 | tf_op jit(solution)/shard_map/reduce_scatter | solution.py:16
  1099.3 22.9 %all_to_all.147 = f32[8,1,40960]{2,1,0:T(1,128)S(1)} all-to-all(f32[8,1,40960]{2,1,0:T(1,128)S(1)} %reshape.125), channel_id=1, replica_groups=mesh['case'=1,'model'=4,'ens'=8] {'ens'}, dimensions={0} | all-to-all | bytes 2621440 | tf_op jit(solution)/shard_map/all_to_all | solution.py:50
  1154.2 19.5 %all_to_all.148 = f32[4,1,81920]{2,1,0:T(1,128)S(1)} all-to-all(f32[4,1,81920]{2,1,0:T(1,128)S(1)} %reshape.127), channel_id=1, replica_groups=mesh['case'=1,'model'=4,'ens'=8] {'model'}, dimensions={0} | all-to-all | bytes 2621440 | tf_op jit(solution)/shard_map/all_to_all | solution.py:51
  1358.0 26.6 %all_to_all.149 = f32[160,32,64]{0,1,2:T(8,128)S(1)} all-to-all(f32[160,32,64]{0,1,2:T(8,128)S(1)} %copy.185), channel_id=1, replica_groups=mesh['case'=1,'model'=4,'ens'=8] {'model'}, dimensions={2} | all-to-all | bytes 2621440 | tf_op jit(solution)/shard_map/all_to_all | solution.py:54
  1387.3 23.5 %all_to_all.150 = f32[640,32,16]{0,2,1:T(8,128)S(1)} all-to-all(f32[640,32,16]{0,2,1:T(8,128)S(1)} %all_to_all.131), channel_id=1, replica_groups=mesh['case'=1,'model'=4,'ens'=8] {'ens'}, dimensions={1} | all-to-all | bytes 2621440 | tf_op jit(solution)/shard_map/all_to_all | solution.py:55
  (213 shorter events, 491.3 us)
Async XLA Ops:
  6.5 63.1 %all-gather.7.cloned.1.call-start = ((), (), s32[]{:S(2)}) async-start(), calls=%async_computation.14 | async-start | bytes 3276800 | tf_op jit(solution)/shard_map/all_gather | solution.py:13
  32.5 37.1 %copy-start.17 = (bf16[3,256,64]{1,2,0:T(8,128)(2,1)S(1)}, bf16[3,256,64]{1,2,0:T(8,128)(2,1)}, u32[]{:S(2)}) copy-start(bf16[3,256,64]{1,2,0:T(8,128)(2,1)} %param.15) | copy-start | bytes 294916
  32.5 37.1 %copy-start.18 = (bf16[3,64,256]{2,1,0:T(8,128)(2,1)S(1)}, bf16[3,64,256]{2,1,0:T(8,128)(2,1)}, u32[]{:S(2)}) copy-start(bf16[3,64,256]{2,1,0:T(8,128)(2,1)} %param.14) | copy-start | bytes 294916
  33.5 102.7 %reduce-scatter.7.cloned.1.call-start = ((), (), s32[]{:S(2)}) async-start(), calls=%async_computation.15 | async-start | bytes 6553600 | tf_op jit(solution)/shard_map/reduce_scatter | solution.py:16
  82.9 53.3 %copy-start.2 = (f32[4,5120,16]{1,2,0:T(8,128)S(1)}, f32[4,5120,16]{1,2,0:T(8,128)}, u32[]{:S(2)}) copy-start(f32[4,5120,16]{1,2,0:T(8,128)} %param.12) | copy-start | bytes 3932164
  82.9 108.4 %all-gather.9.cloned.1.call-start = ((), (), s32[]{:S(2)}) async-start(), calls=%async_computation.16 | async-start | bytes 3276800 | tf_op jit(solution)/shard_map/all_gather | solution.py:13
  159.2 98.7 %reduce-scatter.9.cloned.1.call-start = ((), (), s32[]{:S(2)}) async-start(), calls=%async_computation.17 | async-start | bytes 6553600 | tf_op jit(solution)/shard_map/reduce_scatter | solution.py:16
  204.6 53.3 %copy-start.3 = (f32[5120,4,16]{0,2,1:T(8,128)S(1)}, f32[5120,4,16]{0,2,1:T(8,128)}, u32[]{:S(2)}) copy-start(f32[5120,4,16]{0,2,1:T(8,128)} %reduce-scatter.7.cloned.1.call-done) | copy-start | bytes 3932164
  204.6 108.4 %all-gather.11.cloned.1.call-start = ((), (), s32[]{:S(2)}) async-start(), calls=%async_computation.18 | async-start | bytes 3276800 | tf_op jit(solution)/shard_map/all_gather | solution.py:13
  280.9 98.7 %reduce-scatter.11.cloned.1.call-start = ((), (), s32[]{:S(2)}) async-start(), calls=%async_computation.19 | async-start | bytes 6553600 | tf_op jit(solution)/shard_map/reduce_scatter | solution.py:16
  457.4 4.8 copy-start.20
  457.4 20.3 %all-to-all-start.1 = ((f32[4,1,81920]{2,1,0:T(1,128)}), f32[4,1,81920]{2,1,0:T(1,128)S(1)}, u32[]{:S(2)}, u32[]{:S(2)}) async-start(f32[4,1,81920]{2,1,0:T(1,128)} %reshape.123), calls=%async_computation.4 | async-start | bytes 2621440 | tf_op jit(solution)/shard_map/all_to_all | solution.py:51
  461.2 306.8 %all-gather.13.cloned.1.call-start = ((), (), s32[]{:S(2)}) async-start(), calls=%async_computation.20 | async-start | bytes 3276800 | tf_op jit(solution)/shard_map/all_gather | solution.py:13
  462.2 55.2 %copy-start.12 = (pred[32,32]{1,0:T(8,128)(4,1)}, pred[32,32]{1,0:T(8,128)(4,1)S(1)}, u32[]{:S(2)}) copy-start(pred[32,32]{1,0:T(8,128)(4,1)S(1)} %iota_compare_fusion) | copy-start | bytes 3076
  462.2 41.8 %copy-start.14 = (s32[1024]{0:T(1024)}, s32[1024]{0:T(1024)S(1)}, u32[]{:S(2)}) copy-start(s32[1024]{0:T(1024)S(1)} %pad_clamp_fusion) | copy-start | bytes 12292
  462.3 69.6 %copy-start.6 = (f32[32,32]{1,0:T(8,128)}, f32[32,32]{1,0:T(8,128)S(1)}, u32[]{:S(2)}) copy-start(f32[32,32]{1,0:T(8,128)S(1)} %get-tuple-element.15) | copy-start | bytes 12292
  462.3 177.4 %copy-start = (f32[32,32]{1,0:T(8,128)}, f32[32,32]{1,0:T(8,128)S(1)}, u32[]{:S(2)}) copy-start(f32[32,32]{1,0:T(8,128)S(1)} %get-tuple-element.16) | copy-start | bytes 12292
  462.3 166.7 %copy-start.15 = (pred[32]{0:T(512)(128)(4,1)}, pred[32]{0:T(512)(128)(4,1)S(1)}, u32[]{:S(2)}) copy-start(pred[32]{0:T(512)(128)(4,1)S(1)} %compare_and_fusion) | copy-start | bytes 100
  624.6 4.3 copy-start.10
  629.2 6.1 copy-start.5
  714.8 53.2 %copy-start.19 = (bf16[3,64,256]{2,1,0:T(8,128)(2,1)S(1)}, bf16[3,64,256]{2,1,0:T(8,128)(2,1)}, u32[]{:S(2)}) copy-start(bf16[3,64,256]{2,1,0:T(8,128)(2,1)} %param.14) | copy-start | bytes 294916
  737.8 96.8 %reduce-scatter.13.cloned.1.call-start = ((), (), s32[]{:S(2)}) async-start(), calls=%async_computation.21 | async-start | bytes 6553600 | tf_op jit(solution)/shard_map/reduce_scatter | solution.py:16
  781.3 109.8 %all-gather.15.cloned.1.call-start = ((), (), s32[]{:S(2)}) async-start(), calls=%async_computation.22 | async-start | bytes 3276800 | tf_op jit(solution)/shard_map/all_gather | solution.py:13
  859.0 98.7 %reduce-scatter.15.cloned.1.call-start = ((), (), s32[]{:S(2)}) async-start(), calls=%async_computation.23 | async-start | bytes 6553600 | tf_op jit(solution)/shard_map/reduce_scatter | solution.py:16
  904.4 109.8 %all-gather.17.cloned.1.call-start = ((), (), s32[]{:S(2)}) async-start(), calls=%async_computation.24 | async-start | bytes 3276800 | tf_op jit(solution)/shard_map/all_gather | solution.py:13
  982.2 98.7 %reduce-scatter.17.cloned.1.call-start = ((), (), s32[]{:S(2)}) async-start(), calls=%async_computation.25 | async-start | bytes 6553600 | tf_op jit(solution)/shard_map/reduce_scatter | solution.py:16
  1200.0 3.3 copy-start.16
  1209.6 3.9 copy-start.7
  1209.6 3.9 copy-start.13
  1213.6 7.2 copy-start.1
  1320.8 4.3 copy-start.11
  1325.3 6.1 copy-start.4
  (2 other events, 6.5 us)
Sparse Core Ops, SparseCore 0:
  33.6 35.9 all-gather.6
  83.1 53.0 reduce-scatter.6
  159.3 31.9 all-gather.8
  204.8 53.0 reduce-scatter.8
  281.0 31.9 all-gather.10
  326.5 53.0 reduce-scatter.10
  737.9 30.0 all-gather.12
  781.4 53.0 reduce-scatter.12
  859.1 31.9 all-gather.14
  904.6 53.0 reduce-scatter.14
  982.3 31.9 all-gather.16
  1027.7 53.0 reduce-scatter.16
where the time goes:
time: 1430 us; the launch traced here: 1420 us
  waiting for transfers between devices  529 us (37%)
  matrix products  500 us (35%)
  local copies, waits for them, and re-layouts  168 us (12%)
  blocking collectives  165 us (12%)
  other arithmetic  36.2 us (3%)
  between operations  15.3 us (1%)
    reduce_scatter x6, waiting for transfers between devices, value_a8(): lax.psum_scatter(part_sum, 'model', scatter_dimension=2, tiled=True)  318 us
    all_gather x6, waiting for transfers between devices, value_a8(): mix_full = lax.all_gather(mix_out, 'model', axis=2, tiled=True)  194 us
    dot_general x5, matrix products, value_a8(): jnp.einsum('ij,jkc->ikc', mix_op, ens_state.astype(jnp.bfloat16), preferr...  115 us
    dot_general x6, matrix products, value_a8(): jnp.einsum('ikf,fv->ikv', hidden.astype(jnp.bfloat16), w_out[layer_idx],...  79.5 us
    dot_general x22, matrix products, letkf_weights(): z_mat = jnp.matmul(t_mat, z_mat, precision=FULL_PREC)  77.5 us
    dot_general x22, matrix products, letkf_weights(): t_mat = 1.5 * identity - 0.5 * jnp.matmul(z_mat, b_mat, precision=FULL_PREC)  73.4 us
    dot_general x22, matrix products, letkf_weights(): b_mat = jnp.matmul(b_mat, t_mat, precision=FULL_PREC)  73.3 us
    unnamed x50, local copies, waits for them, and re-layouts  61.8 us
  transfers between devices with their start and end apart: 13, of which 13 were waited for; matrix products, arithmetic and copies ran while one was open for 0% of the time, Pallas kernels for 0%

commit v1 on v0

v1 whole, which is shorter than its diff:
```python
import functools

import jax
import jax.numpy as jnp
from jax import lax
from jax.experimental import pallas as pl
from jax.experimental.pallas import tpu as pltpu
from jax.sharding import PartitionSpec as P

NS_STEPS = 12
LANES = 128
SUB = 8
MESH = pl.DeviceIdType.MESH
VMEM = pl.BlockSpec(memory_space=pltpu.VMEM)
SMEM = pl.BlockSpec(memory_space=pltpu.SMEM)


def greet(peers):
    barrier = pltpu.get_barrier_semaphore()
    for peer in peers:
        pl.semaphore_signal(barrier, inc=1, device_id=peer, device_id_type=MESH)
    pl.semaphore_wait(barrier, len(peers))


def gather_vars_kernel(n_model, x_ref, w_ref, u_ref, h_ref, wa_ref, ua_ref, send_sem, recv_sem, own_sem):
    me = lax.axis_index('model')
    others = [lax.rem(me + t, n_model) for t in range(1, n_model)]
    greet([{'model': o} for o in others])
    copies = []
    for t, o in enumerate(others):
        for a, (src, dst) in enumerate(((x_ref.at[o], h_ref.at[me]), (w_ref, wa_ref.at[me]), (u_ref, ua_ref.at[me]))):
            copies.append(pltpu.make_async_remote_copy(src_ref=src, dst_ref=dst, send_sem=send_sem.at[3 * t + a], recv_sem=recv_sem.at[3 * t + a], device_id={'model': o}, device_id_type=MESH))
    for copy in copies:
        copy.start()
    own = [pltpu.make_async_copy(src, dst, own_sem.at[a]) for a, (src, dst) in enumerate(((x_ref.at[me], h_ref.at[me]), (w_ref, wa_ref.at[me]), (u_ref, ua_ref.at[me])))]
    for copy in own:
        copy.start()
    for copy in own + copies:
        copy.wait()


def gather_vars(x, w, u, n_model):
    n_sem = 3 * (n_model - 1)
    return pl.pallas_call(
        functools.partial(gather_vars_kernel, n_model),
        out_shape=(jax.ShapeDtypeStruct(x.shape, x.dtype), jax.ShapeDtypeStruct((n_model,) + w.shape, w.dtype), jax.ShapeDtypeStruct((n_model,) + u.shape, u.dtype)),
        in_specs=[VMEM] * 3,
        out_specs=[VMEM] * 3,
        scratch_shapes=[pltpu.SemaphoreType.DMA((n_sem,)), pltpu.SemaphoreType.DMA((n_sem,)), pltpu.SemaphoreType.DMA((3,))],
        compiler_params=pltpu.CompilerParams(collective_id=0, has_side_effects=True),
        name='gather_vars',
    )(x, w, u)


def exchange_kernel(n_model, n_ens, x_ref, o_ref, send_sem, recv_sem, own_sem):
    my_m, my_e = lax.axis_index('model'), lax.axis_index('ens')
    me = my_e * n_model + my_m
    steps = [(e, m) for e in range(n_ens) for m in range(n_model)][1:]
    peers = [(lax.rem(my_e + e, n_ens), lax.rem(my_m + m, n_model)) for e, m in steps]
    greet([{'ens': e, 'model': m} for e, m in peers])
    copies = []
    for t, (e, m) in enumerate(peers):
        copies.append(pltpu.make_async_remote_copy(src_ref=x_ref.at[e * n_model + m], dst_ref=o_ref.at[me], send_sem=send_sem.at[t], recv_sem=recv_sem.at[t], device_id={'ens': e, 'model': m}, device_id_type=MESH))
    for copy in copies:
        copy.start()
    own = pltpu.make_async_copy(x_ref.at[me], o_ref.at[me], own_sem)
    own.start()
    own.wait()
    for copy in copies:
        copy.wait()


def exchange(x, n_model, n_ens):
    n_sem = n_model * n_ens - 1
    return pl.pallas_call(
        functools.partial(exchange_kernel, n_model, n_ens),
        out_shape=jax.ShapeDtypeStruct(x.shape, x.dtype),
        in_specs=[VMEM],
        out_specs=VMEM,
        scratch_shapes=[pltpu.SemaphoreType.DMA((n_sem,)), pltpu.SemaphoreType.DMA((n_sem,)), pltpu.SemaphoreType.DMA],
        compiler_params=pltpu.CompilerParams(collective_id=1, has_side_effects=True),
        name='exchange',
    )(x)


GELU_C = 0.7978845608028654


def layer_kernel(hb_ref, h_ref, a_ref, wt_ref, ut_ref, ho_ref, hbo_ref):
    mix = lax.dot_general(hb_ref[...], a_ref[...], (((1,), (1,)), ((), ())), preferred_element_type=jnp.float32).astype(jnp.bfloat16)
    half = jnp.dot(wt_ref[...], mix, preferred_element_type=jnp.float32)
    arg = half * (2 * GELU_C + (8 * GELU_C * 0.044715) * (half * half))
    act = half * jnp.tanh(arg) + half
    new = h_ref[...] + jnp.dot(ut_ref[...], act.astype(jnp.bfloat16), preferred_element_type=jnp.float32)
    ho_ref[...] = new
    hbo_ref[...] = new.astype(jnp.bfloat16)


def layer(hb, h, mix_op, wt, ut, block=256):
    n_vars, cols = h.shape
    hidden = wt.shape[0]
    return pl.pallas_call(
        layer_kernel,
        grid=(cols // block,),
        out_shape=(jax.ShapeDtypeStruct(h.shape, jnp.float32), jax.ShapeDtypeStruct(h.shape, jnp.bfloat16)),
        in_specs=[
            pl.BlockSpec((n_vars, cols), lambda i: (0, 0)),
            pl.BlockSpec((n_vars, block), lambda i: (0, i)),
            pl.BlockSpec((block, cols), lambda i: (i, 0)),
            pl.BlockSpec((hidden, n_vars), lambda i: (0, 0)),
            pl.BlockSpec((n_vars, hidden), lambda i: (0, 0)),
        ],
        out_specs=(pl.BlockSpec((n_vars, block), lambda i: (0, i)), pl.BlockSpec((n_vars, block), lambda i: (0, i))),
        cost_estimate=pl.CostEstimate(flops=2 * n_vars * cols * (cols + 2 * hidden), bytes_accessed=2 * cols * cols, transcendentals=hidden * cols),
        name='layer',
    )(hb, h, mix_op, wt, ut)


def lane_pick(lanes, pieces):
    out = pieces[-1][1]
    for bound, piece in reversed(pieces[:-1]):
        out = jnp.where(lanes < bound, piece, out)
    return out


def pack_kernel(rem, h_ref, o_ref):
    fold = LANES // rem
    rows = h_ref.shape[0]
    deep = rows // fold
    span = fold * (LANES + rem)
    lanes = lax.broadcasted_iota(jnp.int32, (rows, LANES), 1)
    dlanes = lax.broadcasted_iota(jnp.int32, (deep, LANES), 1)

    @pl.loop(0, h_ref.shape[1] // span)
    def _(a):
        part = [h_ref[:, pl.ds(pl.multiple_of(a * span + g * LANES, LANES), LANES)] for g in range(fold + 1)]
        for b in range(fold):
            j = a * fold + b
            main = part[0] if b == 0 else pltpu.roll(jnp.where(lanes < rem * b, part[b + 1], part[b]), LANES - rem * b, 1)
            o_ref[j, 0:rows, :] = main
            tail = [part[b + 1][deep * q:deep * (q + 1)] for q in range(fold)]
            tail = [x if q == b else pltpu.roll(x, (rem * (q - b)) % LANES, 1) for q, x in enumerate(tail)]
            o_ref[j, rows:rows + deep, :] = lane_pick(dlanes, [(rem * (q + 1), x) for q, x in enumerate(tail)])


def pack(h, n_blocks):
    rows, cols = h.shape
    rem = cols // n_blocks - LANES
    return pl.pallas_call(
        functools.partial(pack_kernel, rem),
        out_shape=jax.ShapeDtypeStruct((n_blocks, rows + rows * rem // LANES, LANES), h.dtype),
        in_specs=[VMEM],
        out_specs=VMEM,
        name='pack',
    )(h)


def unpack_kernel(rem, rows, x_ref, *outs):
    fold = LANES // rem
    deep = rows // fold
    span = fold * (LANES + rem)
    lanes = lax.broadcasted_iota(jnp.int32, (rows, LANES), 1)

    @pl.loop(0, x_ref.shape[0] // fold)
    def _(a):
        mains, tails = [], []
        for b in range(fold):
            main = x_ref[a * fold + b, 0:rows, :]
            mains.append(main if b == 0 else pltpu.roll(main, rem * b, 1))
            tail = x_ref[a * fold + b, rows:rows + deep, :]
            tails.append(jnp.concatenate([tail if q == b else pltpu.roll(tail, (rem * (b - q)) % LANES, 1) for q in range(fold)], axis=0))
        for g in range(fold + 1):
            if g == 0:
                piece = mains[0]
            else:
                piece = jnp.where(lanes < rem * (g - 1), mains[g - 1], tails[g - 1])
                if g < fold:
                    piece = jnp.where(lanes < rem * g, piece, mains[g])
            for out in outs:
                out[:, pl.ds(pl.multiple_of(a * span + g * LANES, LANES), LANES)] = piece.astype(out.dtype)


def unpack(x, rows, dtypes):
    n_blocks, depth, _ = x.shape
    rem = (depth - rows) * LANES // rows
    return pl.pallas_call(
        functools.partial(unpack_kernel, rem, rows),
        out_shape=tuple(jax.ShapeDtypeStruct((rows, n_blocks * (LANES + rem)), t) for t in dtypes),
        in_specs=[VMEM],
        out_specs=tuple(VMEM for t in dtypes),
        name='unpack',
    )(x)


def analysis_kernel(n_model, by_output, idx_ref, rho_ref, x_ref, y_ref, r_ref, o_ref, xs, xa, mean, mats, yo, gy, vec):
    members, depth, _ = x_ref.shape
    n_vars = mean.shape[0]
    n_obs = y_ref.shape[1]
    rem = (depth - n_vars) * LANES // n_vars
    fold = LANES // rem
    deep = n_vars // fold
    groups = members // SUB
    size = members * members
    part = pl.program_id(0)
    eight = lax.broadcasted_iota(jnp.int32, (SUB, LANES), 0)
    dlanes = lax.broadcasted_iota(jnp.int32, (deep, LANES), 1)

    @pl.when(part == 0)
    def _():
        @pl.loop(0, members)
        def _(k):
            xs[pl.ds(pl.multiple_of(k * n_vars, SUB), n_vars), :] = x_ref[k, 0:n_vars, :]

    @pl.when(part != 0)
    def _():
        @pl.loop(0, members)
        def _(k):
            tail = x_ref[k, n_vars:depth, :]
            for q in range(fold):
                xs[pl.ds(pl.multiple_of(k * n_vars + deep * q, SUB), deep), :] = tail if q == 0 else pltpu.roll(tail, LANES - rem * q, 1)

    total = xs[0:n_vars, :]
    for k in range(1, members):
        total = total + xs[k * n_vars:(k + 1) * n_vars, :]
    mean[...] = total * (1.0 / members)

    @pl.loop(0, n_vars)
    def _(v):
        xa[pl.ds(pl.multiple_of(v * members, SUB), members), :] = xs[pl.ds(v, members, stride=n_vars), :] - mean[pl.ds(v, 1), :]

    @pl.loop(0, n_obs)
    def _(p):
        var = idx_ref[p]
        row = pl.multiple_of(p * members, SUB)
        here = xa[pl.ds(pl.multiple_of(var * members, SUB), members), :]
        yo[pl.ds(row, members), :] = here
        gy[pl.ds(row, members), :] = here * r_ref[0, pl.ds(p, 1), :]
        vec[pl.ds(p, 1), :] = y_ref[0, pl.ds(p, 1), :] - mean[pl.ds(var, 1), :]

    def product(left, left_at, right, right_at, out, out_at, scale, diag):
        for i in range(groups):
            wide = members - SUB * i

            def body(kk, acc):
                for k4 in range(4):
                    k = (kk * 4 + k4) * members + SUB * i
                    r = right[pl.ds(pl.multiple_of(right_at + k, SUB), wide), :]
                    acc = tuple(acc[a] + left[pl.ds(left_at + k + a, 1), :] * r for a in range(SUB))
                return acc

            acc = lax.fori_loop(0, members // 4, body, tuple(jnp.zeros((wide, LANES), jnp.float32) for a in range(SUB)))
            for a in range(SUB):
                val = acc[a] if scale is None else acc[a] * scale
                first = val[0:SUB]
                if diag is not None:
                    first = first + jnp.where(eight == a, diag, 0.0)
                out[pl.ds(pl.multiple_of(out_at + (SUB * i + a) * members + SUB * i, SUB), SUB), :] = first
                if i + 1 < groups:
                    out[pl.ds(pl.multiple_of(out_at + (SUB * i + a) * members + SUB * (i + 1), SUB), wide - SUB), :] = val[SUB:]
                    out[pl.ds(out_at + SUB * (i + 1) * members + SUB * i + a, wide - SUB, stride=members), :] = val[SUB:]

    slot = lambda s: pl.multiple_of(lax.rem(s + 4 * NS_STEPS, 4) * size, SUB)
    product(gy, 0, yo, 0, mats, slot(3), None, (members - 1) / rho_ref[0])
    trace = jnp.sum(mats[pl.ds(slot(3), members, stride=members + 1), :], axis=0, keepdims=True)
    inv = 1.0 / trace

    @pl.loop(0, members)
    def _(i):
        row = pl.multiple_of(i * members, SUB)
        b = mats[pl.ds(slot(3) + row, members), :] * inv
        eye = jnp.where(lax.broadcasted_iota(jnp.int32, (members, LANES), 0) == i, 1.5, 0.0)
        t = eye - 0.5 * b
        mats[pl.ds(slot(0) + row, members), :] = b
        mats[pl.ds(slot(1) + row, members), :] = t
        mats[pl.ds(slot(2) + row, members), :] = t

    def step(s, carry):
        b, t, z, n = slot(-s), slot(1 - s), slot(2 - s), slot(3 - s)
        product(mats, b, mats, t, mats, n, None, None)
        product(mats, z, mats, n, mats, b, -0.5, 1.5)
        product(mats, b, mats, z, mats, t, None, None)
        return carry

    lax.fori_loop(0, NS_STEPS - 1, step, 0)
    z = slot(2 - (NS_STEPS - 1))
    root = 1.0 / jnp.sqrt(trace)

    def weighted(left, at, base, scale):
        acc = jnp.zeros((members, LANES), jnp.float32)
        for p in range(left.shape[0] // members if left is not mats else members):
            acc = acc + left[pl.ds(at + p * members, members), :] * vec[base + p:base + p + 1, :]
        return acc if scale is None else acc * scale

    vec[n_obs:n_obs + members, :] = weighted(gy, 0, 0, None)
    vec[n_obs + members:n_obs + 2 * members, :] = weighted(mats, z, n_obs, root)
    vec[n_obs:n_obs + members, :] = weighted(mats, z, n_obs + members, root)

    @pl.loop(0, members)
    def _(i):
        row = pl.multiple_of(i * members, SUB)
        gy[pl.ds(row, members), :] = mats[pl.ds(z + row, members), :] * (root * (members - 1) ** 0.5) + vec[pl.ds(n_obs + i, 1), :]

    @pl.loop(0, n_vars // 4)
    def _(v4):
        acc = [jnp.broadcast_to(mean[pl.ds(v4 * 4 + c, 1), :], (members, LANES)) for c in range(4)]

        def body(ii, acc):
            for i4 in range(4):
                i = ii * 4 + i4
                wa = gy[pl.ds(pl.multiple_of(i * members, SUB), members), :]
                acc = tuple(acc[c] + xa[pl.ds((v4 * 4 + c) * members + i, 1), :] * wa for c in range(4))
            return acc

        acc = lax.fori_loop(0, members // 4, body, tuple(acc))
        for c in range(4):
            xs[pl.ds(v4 * 4 + c, members, stride=n_vars), :] = acc[c]

    def source(dest, q):
        if by_output:
            return pl.multiple_of((dest // n_model * n_model + q) * n_vars + dest % n_model * deep, SUB)
        return pl.multiple_of(dest * n_vars + q * deep, SUB)

    @pl.when(part == 0)
    def _():
        @pl.loop(0, members)
        def _(dest):
            for q in range(fold):
                o_ref[dest, deep * q:deep * (q + 1), :] = xs[pl.ds(source(dest, q), deep), :]

    @pl.when(part != 0)
    def _():
        @pl.loop(0, members)
        def _(dest):
            tail = [xs[pl.ds(source(dest, q), deep), :] for q in range(fold)]
            tail = [x if q == 0 else pltpu.roll(x, rem * q, 1) for q, x in enumerate(tail)]
            o_ref[dest, n_vars:depth, :] = lane_pick(dlanes, [(rem * (q + 1), x) for q, x in enumerate(tail)])


def analysis(x, y, r, obs_idx, inflation, n_vars, n_model, by_output):
    members, depth, _ = x.shape
    parts, n_obs, _ = y.shape
    whole = pl.BlockSpec(x.shape, lambda g: (0, 0, 0))
    obs = pl.BlockSpec((1, n_obs, LANES), lambda g: (g, 0, 0))
    return pl.pallas_call(
        functools.partial(analysis_kernel, n_model, by_output),
        grid=(parts,),
        out_shape=jax.ShapeDtypeStruct(x.shape, jnp.float32),
        in_specs=[SMEM, SMEM, whole, obs, obs],
        out_specs=whole,
        scratch_shapes=[
            pltpu.VMEM((members * n_vars, LANES), jnp.float32),
            pltpu.VMEM((members * n_vars, LANES), jnp.float32),
            pltpu.VMEM((n_vars, LANES), jnp.float32),
            pltpu.VMEM((4 * members * members, LANES), jnp.float32),
            pltpu.VMEM((n_obs * members, LANES), jnp.float32),
            pltpu.VMEM((n_obs * members, LANES), jnp.float32),
            pltpu.VMEM((n_obs + 2 * members, LANES), jnp.float32),
        ],
        name='analysis',
    )(obs_idx, inflation, x, y, r)


def by_lanes(x, fill):
    x = jnp.swapaxes(x, -1, -2)
    pad = -x.shape[-1] % LANES
    x = jnp.pad(x, [(0, 0)] * (x.ndim - 1) + [(0, pad)], constant_values=fill)
    return jnp.moveaxis(x.reshape(x.shape[:-1] + (-1, LANES)), -2, -3)


def solution(mesh):
    n_model, n_ens = mesh.shape['model'], mesh.shape['ens']

    def local_step(ens_local, mix_op, w_in, w_out, obs_val, obs_prec, obs_idx, inflation):
        held, cols, own_vars = ens_local.shape
        n_blocks = n_model * n_ens
        cycles, layers, n_vars = obs_val.shape[0], w_in.shape[0], w_in.shape[1]
        x = jnp.swapaxes(ens_local, 1, 2)
        h, w_all, u_all = gather_vars(x, w_in, jnp.swapaxes(w_out, 1, 2), n_model)
        h = h.reshape(n_vars, cols)
        hb = h.astype(jnp.bfloat16)
        wt = (jnp.transpose(w_all, (1, 0, 3, 2)) * jnp.bfloat16(0.5)).reshape(layers, -1, n_vars)
        ut = jnp.transpose(u_all, (1, 2, 0, 3)).reshape(layers, n_vars, -1)
        y = by_lanes(obs_val, 0.0)
        r = by_lanes(obs_prec, 1.0)
        for cycle in range(cycles):
            last = cycle + 1 == cycles
            for n in range(layers):
                h, hb = layer(hb, h, mix_op, wt[n], ut[n])
            x = exchange(pack(h, n_blocks), n_model, n_ens)
            x = analysis(x, y[cycle], r, obs_idx, inflation, n_vars, n_model, last)
            x = exchange(x, n_model, n_ens)
            if last:
                (h,) = unpack(x, n_vars, (jnp.float32,))
            else:
                h, hb = unpack(x, n_vars, (jnp.float32, jnp.bfloat16))
        return jnp.swapaxes(h.reshape(held, own_vars, cols), 1, 2)

    member_spec = P(('case', 'ens'), None, 'model')
    col_axes = ('case', 'ens', 'model')
    in_specs = (member_spec, P(None, None), P(None, None, 'model'), P(None, 'model', None), P(None, col_axes, None), P(col_axes, None), P(None), P(None))
    return jax.shard_map(local_step, mesh=mesh, in_specs=in_specs, out_specs=member_spec, check_vma=False)
```

time: 1430 us -> 574 us (0.40)
  Pallas kernels: 0 us -> 560 us
  waiting for transfers between devices: 529 us -> 0 us
  matrix products: 500 us -> 0 us
  blocking collectives: 165 us -> 0 us
  local copies, waits for them, and re-layouts: 168 us -> 6.17 us
  other arithmetic: 36.2 us -> 2 us
  between operations: 15.3 us -> 0.76 us
    pallas_call x0 -> x17, Pallas kernels: none -> 560 us  [the longest x6 224 us: layer(): pl.pallas_call(layer_kernel, grid=(cols // block,), out_shape=(jax.ShapeD...]
    dot_general x87 -> x0, matrix products: 475 us -> none  [the longest x5 115 us: value_a8(): jnp.einsum('ij,jkc->ikc', mix_op, ens_state.astype(jnp.bfloat16), preferr...]
    reduce_scatter x6 -> x0, waiting for transfers between devices: 318 us -> none  [value_a8(): lax.psum_scatter(part_sum, 'model', scatter_dimension=2, tiled=True)]
    all_gather x6 -> x0, waiting for transfers between devices: 194 us -> none  [value_a8(): mix_full = lax.all_gather(mix_out, 'model', axis=2, tiled=True)]
    all_to_all x7 -> x0, blocking collectives: 165 us -> none  [the longest x2 53 us: local_step(): col_state = lax.all_to_all(col_state, 'model', 2, 0, tiled=True)]
    unnamed x50 -> x11, local copies, waits for them, and re-layouts: 61.8 us -> 2 us
    all_to_all x17 -> x0, local copies, waits for them, and re-layouts: 52.9 us -> none  [the longest x5 25.2 us: local_step(): col_state = lax.all_to_all(ens_state, 'ens', 0, 1, tiled=True)]
    unnamed x1 -> x0, matrix products: 24.5 us -> none
  transfers between devices with their start and end apart: 13 -> 0, of which waited for: 13 -> 0; matrix products, arithmetic and copies ran while one was open for 0% -> 0% of each run, Pallas kernels for 0% -> 0%
where the time goes in v1:
time: 574 us; the launch traced here: 569 us
  Pallas kernels  560 us (98%)
  local copies, waits for them, and re-layouts  6.17 us (1%)
    pallas_call x6, Pallas kernels, layer(): pl.pallas_call(layer_kernel, grid=(cols // block,), out_shape=(jax.ShapeD...  224 us
    pallas_call x2, Pallas kernels, analysis(): pl.pallas_call(functools.partial(analysis_kernel, n_model, by_output), gr...  191 us
    pallas_call x4, Pallas kernels, exchange(): pl.pallas_call(functools.partial(exchange_kernel, n_model, n_ens), out_sh...  100 us
    pallas_call x1, Pallas kernels, gather_vars(): pl.pallas_call(functools.partial(gather_vars_kernel, n_model), out_shape=...  31.9 us

profile of v1, /device:TPU:97, one launch (start us, length us, event | category | flops | bytes accessed | tf_op | source)
XLA Modules:
  0.0 569.0 jit_solution(7616604689661320990)
XLA Ops:
  0.0 31.9 %gather_vars.1 = (f32[4,16,5120]{2,1,0:T(8,128)}, bf16[4,3,64,256]{3,2,1,0:T(8,128)(2,1)}, bf16[4,3,64,256]{3,2,1,0:T(8,128)(2,1)}) custom-call(f32[4,16,5120]{2,1,0:T(8,128)} %bitcast.49, bf16[3,64,256]{2,1,0:T(8,128)(2,1)} %w_ref.1, bf16[3,64,256]{2,1,0:T(8,128)(2,1)} %bitcast.60), custom_call_target="tpu_custom_call" | custom-call | tf_op jit(solution)/shard_map/gather_vars/pallas_call | solution.py:44
  31.9 1.1 multiply_bitcast_fusion
  33.0 0.0 copy-start
  33.1 0.8 copy.15
  33.9 0.1 copy.16
  34.1 0.7 copy.25
  34.7 0.9 bitcast_convert_fusion.hb_ref
  35.6 37.3 %layer.6 = (f32[64,5120]{1,0:T(8,128)}, bf16[64,5120]{1,0:T(8,128)(2,1)}) custom-call(bf16[64,5120]{1,0:T(8,128)(2,1)} %bitcast_convert_fusion.hb_ref, f32[64,5120]{1,0:T(8,128)} %bitcast.42, bf16[5120,5120]{1,0:T(8,128)(2,1)} %a_ref.11, bf16[1024,64]{1,0:T(8,128)(2,1)} %bitcast.43, bf16[64,1024]{1,0:T(8,128)(2,1)} %bitcast.50), custom_call_target="tpu_custom_call" | custom-call | flops 4697620480 | bytes 52428800 | tf_op jit(solution)/shard_map/layer/pallas_call | solution.py:102
  72.9 0.8 copy.17
  73.7 0.1 copy.18
  73.8 0.7 copy.26
  74.5 37.3 %layer.7 = (f32[64,5120]{1,0:T(8,128)}, bf16[64,5120]{1,0:T(8,128)(2,1)}) custom-call(bf16[64,5120]{1,0:T(8,128)(2,1)} %get-tuple-element.23.hb_ref, f32[64,5120]{1,0:T(8,128)} %get-tuple-element.24.h_ref, bf16[5120,5120]{1,0:T(8,128)(2,1)} %a_ref.11, bf16[1024,64]{1,0:T(8,128)(2,1)} %bitcast.45, bf16[64,1024]{1,0:T(8,128)(2,1)} %bitcast.52), custom_call_target="tpu_custom_call" | custom-call | flops 4697620480 | bytes 52428800 | tf_op jit(solution)/shard_map/layer/pallas_call | solution.py:102
  111.8 0.9 copy.19
  112.6 0.1 copy.20
  112.7 0.7 copy.27
  113.4 37.3 %layer.8 = (f32[64,5120]{1,0:T(8,128)}, bf16[64,5120]{1,0:T(8,128)(2,1)}) custom-call(bf16[64,5120]{1,0:T(8,128)(2,1)} %get-tuple-element.25.hb_ref, f32[64,5120]{1,0:T(8,128)} %get-tuple-element.26.h_ref, bf16[5120,5120]{1,0:T(8,128)(2,1)} %a_ref.11, bf16[1024,64]{1,0:T(8,128)(2,1)} %bitcast.47, bf16[64,1024]{1,0:T(8,128)(2,1)} %bitcast.54), custom_call_target="tpu_custom_call" | custom-call | flops 4697620480 | bytes 52428800 | tf_op jit(solution)/shard_map/layer/pallas_call | solution.py:102
  150.7 3.4 pack.2.x_ref
  154.0 26.8 %exchange.4.x_ref = f32[32,80,128]{2,1,0:T(8,128)} custom-call(f32[32,80,128]{2,1,0:T(8,128)} %pack.2.x_ref), custom_call_target="tpu_custom_call" | custom-call | tf_op jit(solution)/shard_map/exchange/pallas_call | solution.py:75
  180.8 0.6 slice_bitcast_fusion
  181.5 0.0 copy-done.3
  181.5 0.6 bitcast_bitcast_fusion.1.r_ref
  182.7 95.2 %analysis.2.x_ref = f32[32,80,128]{2,1,0:T(8,128)} custom-call(s32[32]{0:T(128)} %idx_ref.3, f32[1]{0:T(128)S(6)} %copy.30.rho_ref, f32[32,80,128]{2,1,0:T(8,128)} %exchange.4.x_ref, f32[2,32,128]{2,1,0:T(8,128)} %get-tuple-element.42.y_ref, f32[2,32,128]{2,1,0:T(8,128)} %bitcast_bitcast_fusion.1.r_ref), custom_call_target="tpu_custom_call" | custom-call | tf_op jit(solution)/shard_map/analysis/pallas_call | solution.py:344
  277.9 24.4 %exchange.5.x_ref = f32[32,80,128]{2,1,0:T(8,128)} custom-call(f32[32,80,128]{2,1,0:T(8,128)} %analysis.2.x_ref), custom_call_target="tpu_custom_call" | custom-call | tf_op jit(solution)/shard_map/exchange/pallas_call | solution.py:75
  302.4 3.6 unpack.2
  305.9 37.3 %layer.9 = (f32[64,5120]{1,0:T(8,128)}, bf16[64,5120]{1,0:T(8,128)(2,1)}) custom-call(bf16[64,5120]{1,0:T(8,128)(2,1)} %get-tuple-element.28.hb_ref, f32[64,5120]{1,0:T(8,128)} %get-tuple-element.29.h_ref, bf16[5120,5120]{1,0:T(8,128)(2,1)} %a_ref.11, bf16[1024,64]{1,0:T(8,128)(2,1)} %bitcast.44, bf16[64,1024]{1,0:T(8,128)(2,1)} %bitcast.51), custom_call_target="tpu_custom_call" | custom-call | flops 4697620480 | bytes 52428800 | tf_op jit(solution)/shard_map/layer/pallas_call | solution.py:102
  343.2 37.3 %layer.10 = (f32[64,5120]{1,0:T(8,128)}, bf16[64,5120]{1,0:T(8,128)(2,1)}) custom-call(bf16[64,5120]{1,0:T(8,128)(2,1)} %get-tuple-element.30.hb_ref, f32[64,5120]{1,0:T(8,128)} %get-tuple-element.31.h_ref, bf16[5120,5120]{1,0:T(8,128)(2,1)} %a_ref.11, bf16[1024,64]{1,0:T(8,128)(2,1)} %bitcast.46, bf16[64,1024]{1,0:T(8,128)(2,1)} %bitcast.53), custom_call_target="tpu_custom_call" | custom-call | flops 4697620480 | bytes 52428800 | tf_op jit(solution)/shard_map/layer/pallas_call | solution.py:102
  380.5 37.3 %layer.11 = (f32[64,5120]{1,0:T(8,128)}, bf16[64,5120]{1,0:T(8,128)(2,1)}) custom-call(bf16[64,5120]{1,0:T(8,128)(2,1)} %get-tuple-element.32.hb_ref, f32[64,5120]{1,0:T(8,128)} %get-tuple-element.33.h_ref, bf16[5120,5120]{1,0:T(8,128)(2,1)} %a_ref.11, bf16[1024,64]{1,0:T(8,128)(2,1)} %bitcast.48, bf16[64,1024]{1,0:T(8,128)(2,1)} %bitcast.55), custom_call_target="tpu_custom_call" | custom-call | flops 4697620480 | bytes 52428800 | tf_op jit(solution)/shard_map/layer/pallas_call | solution.py:102
  417.8 3.4 pack.3.x_ref
  421.1 23.4 %exchange.6.x_ref = f32[32,80,128]{2,1,0:T(8,128)} custom-call(f32[32,80,128]{2,1,0:T(8,128)} %pack.3.x_ref), custom_call_target="tpu_custom_call" | custom-call | tf_op jit(solution)/shard_map/exchange/pallas_call | solution.py:75
  444.6 95.5 %analysis.3.x_ref = f32[32,80,128]{2,1,0:T(8,128)} custom-call(s32[32]{0:T(128)} %idx_ref.3, f32[1]{0:T(128)S(6)} %copy.30.rho_ref, f32[32,80,128]{2,1,0:T(8,128)} %exchange.6.x_ref, f32[2,32,128]{2,1,0:T(8,128)} %get-tuple-element.41.y_ref, f32[2,32,128]{2,1,0:T(8,128)} %bitcast_bitcast_fusion.1.r_ref), custom_call_target="tpu_custom_call" | custom-call | tf_op jit(solution)/shard_map/analysis/pallas_call | solution.py:344
  540.1 25.5 %exchange.7.x_ref = f32[32,80,128]{2,1,0:T(8,128)} custom-call(f32[32,80,128]{2,1,0:T(8,128)} %analysis.3.x_ref), custom_call_target="tpu_custom_call" | custom-call | tf_op jit(solution)/shard_map/exchange/pallas_call | solution.py:75
  565.6 3.3 unpack.3
  (9 shorter events, 0.1 us)
Async XLA Ops:
  31.9 2.0 copy-start.1
  33.0 1.7 copy-start
  154.0 26.8 %copy-start.2 = (f32[2,160,32]{1,2,0:T(8,128)S(1)}, f32[2,160,32]{1,2,0:T(8,128)}, u32[]{:S(2)}) copy-start(f32[2,160,32]{1,2,0:T(8,128)} %param.12) | copy-start | bytes 122884
  154.0 27.4 %copy-start.3 = (f32[160,32]{0,1:T(8,128)S(1)}, f32[160,32]{0,1:T(8,128)}, u32[]{:S(2)}) copy-start(f32[160,32]{0,1:T(8,128)} %param.13) | copy-start | bytes 61444

commit v2 on v1

v2 whole, which is shorter than its diff:
```python
import functools

import jax
import jax.numpy as jnp
from jax import lax
from jax.experimental import pallas as pl
from jax.experimental.pallas import tpu as pltpu
from jax.sharding import PartitionSpec as P

NS_STEPS = 12
PASSES = ((0,), (1,), (2, 3))
LANES = 128
BLOCK = 256
VMEM_LIMIT = 66_500_000
GELU_C = 0.7978845608028654
SUB = 8
MESH = pl.DeviceIdType.MESH
VMEM = pl.BlockSpec(memory_space=pltpu.VMEM)
SMEM = pl.BlockSpec(memory_space=pltpu.SMEM)


def greet(peers):
    barrier = pltpu.get_barrier_semaphore()
    for peer in peers:
        pl.semaphore_signal(barrier, inc=1, device_id=peer, device_id_type=MESH)
    pl.semaphore_wait(barrier, len(peers))


def gather_vars_kernel(n_model, x_ref, w_ref, u_ref, h_ref, wa_ref, ua_ref, send_sem, recv_sem, own_sem):
    me = lax.axis_index('model')
    others = [lax.rem(me + t, n_model) for t in range(1, n_model)]
    greet([{'model': o} for o in others])
    copies = []
    for t, o in enumerate(others):
        for a, (src, dst) in enumerate(((x_ref.at[o], h_ref.at[me]), (w_ref, wa_ref.at[me]), (u_ref, ua_ref.at[me]))):
            copies.append(pltpu.make_async_remote_copy(src_ref=src, dst_ref=dst, send_sem=send_sem.at[3 * t + a], recv_sem=recv_sem.at[3 * t + a], device_id={'model': o}, device_id_type=MESH))
    for copy in copies:
        copy.start()
    own = [pltpu.make_async_copy(src, dst, own_sem.at[a]) for a, (src, dst) in enumerate(((x_ref.at[me], h_ref.at[me]), (w_ref, wa_ref.at[me]), (u_ref, ua_ref.at[me])))]
    for copy in own:
        copy.start()
    for copy in own + copies:
        copy.wait()


def gather_vars(x, w, u, n_model):
    n_sem = 3 * (n_model - 1)
    return pl.pallas_call(
        functools.partial(gather_vars_kernel, n_model),
        out_shape=(jax.ShapeDtypeStruct(x.shape, x.dtype), jax.ShapeDtypeStruct((n_model,) + w.shape, w.dtype), jax.ShapeDtypeStruct((n_model,) + u.shape, u.dtype)),
        in_specs=[VMEM] * 3,
        out_specs=[VMEM] * 3,
        scratch_shapes=[pltpu.SemaphoreType.DMA((n_sem,)), pltpu.SemaphoreType.DMA((n_sem,)), pltpu.SemaphoreType.DMA((3,))],
        compiler_params=pltpu.CompilerParams(collective_id=0, has_side_effects=True),
        name='gather_vars',
    )(x, w, u)


def exchange_kernel(n_model, n_ens, x_ref, o_ref, send_sem, recv_sem, own_sem):
    my_m, my_e = lax.axis_index('model'), lax.axis_index('ens')
    me = my_e * n_model + my_m
    steps = [(e, m) for e in range(n_ens) for m in range(n_model)][1:]
    peers = [(lax.rem(my_e + e, n_ens), lax.rem(my_m + m, n_model)) for e, m in steps]
    greet([{'ens': e, 'model': m} for e, m in peers])
    copies = []
    for t, (e, m) in enumerate(peers):
        copies.append(pltpu.make_async_remote_copy(src_ref=x_ref.at[e * n_model + m], dst_ref=o_ref.at[me], send_sem=send_sem.at[t], recv_sem=recv_sem.at[t], device_id={'ens': e, 'model': m}, device_id_type=MESH))
    for copy in copies:
        copy.start()
    own = pltpu.make_async_copy(x_ref.at[me], o_ref.at[me], own_sem)
    own.start()
    own.wait()
    for copy in copies:
        copy.wait()


def exchange(x, n_model, n_ens):
    n_sem = n_model * n_ens - 1
    return pl.pallas_call(
        functools.partial(exchange_kernel, n_model, n_ens),
        out_shape=jax.ShapeDtypeStruct(x.shape, x.dtype),
        in_specs=[VMEM],
        out_specs=VMEM,
        scratch_shapes=[pltpu.SemaphoreType.DMA((n_sem,)), pltpu.SemaphoreType.DMA((n_sem,)), pltpu.SemaphoreType.DMA],
        compiler_params=pltpu.CompilerParams(collective_id=1, has_side_effects=True),
        name='exchange',
    )(x)


def lane_pick(lanes, pieces):
    out = pieces[-1][1]
    for bound, piece in reversed(pieces[:-1]):
        out = jnp.where(lanes < bound, piece, out)
    return out


def pack_kernel(rem, h_ref, o_ref):
    fold = LANES // rem
    rows = h_ref.shape[0]
    deep = rows // fold
    span = fold * (LANES + rem)
    lanes = lax.broadcasted_iota(jnp.int32, (rows, LANES), 1)
    dlanes = lax.broadcasted_iota(jnp.int32, (deep, LANES), 1)

    @pl.loop(0, h_ref.shape[1] // span)
    def _(a):
        part = [h_ref[:, pl.ds(pl.multiple_of(a * span + g * LANES, LANES), LANES)] for g in range(fold + 1)]
        for b in range(fold):
            j = a * fold + b
            main = part[0] if b == 0 else pltpu.roll(jnp.where(lanes < rem * b, part[b + 1], part[b]), LANES - rem * b, 1)
            o_ref[j, 0:rows, :] = main
            tail = [part[b + 1][deep * q:deep * (q + 1)] for q in range(fold)]
            tail = [x if q == b else pltpu.roll(x, (rem * (q - b)) % LANES, 1) for q, x in enumerate(tail)]
            o_ref[j, rows:rows + deep, :] = lane_pick(dlanes, [(rem * (q + 1), x) for q, x in enumerate(tail)])


def unpack_kernel(rem, rows, x_ref, *outs):
    fold = LANES // rem
    deep = rows // fold
    span = fold * (LANES + rem)
    lanes = lax.broadcasted_iota(jnp.int32, (rows, LANES), 1)

    @pl.loop(0, x_ref.shape[0] // fold)
    def _(a):
        mains, tails = [], []
        for b in range(fold):
            main = x_ref[a * fold + b, 0:rows, :]
            mains.append(main if b == 0 else pltpu.roll(main, rem * b, 1))
            tail = x_ref[a * fold + b, rows:rows + deep, :]
            tails.append(jnp.concatenate([tail if q == b else pltpu.roll(tail, (rem * (b - q)) % LANES, 1) for q in range(fold)], axis=0))
        for g in range(fold + 1):
            if g == 0:
                piece = mains[0]
            else:
                piece = jnp.where(lanes < rem * (g - 1), mains[g - 1], tails[g - 1])
                if g < fold:
                    piece = jnp.where(lanes < rem * g, piece, mains[g])
            for out in outs:
                out[:, pl.ds(pl.multiple_of(a * span + g * LANES, LANES), LANES)] = piece.astype(out.dtype)


def unpack(x, rows, dtypes):
    n_blocks, depth, _ = x.shape
    rem = (depth - rows) * LANES // rows
    return pl.pallas_call(
        functools.partial(unpack_kernel, rem, rows),
        out_shape=tuple(jax.ShapeDtypeStruct((rows, n_blocks * (LANES + rem)), t) for t in dtypes),
        in_specs=[VMEM],
        out_specs=tuple(VMEM for t in dtypes),
        name='unpack',
    )(x)


def forecast_kernel(rem, packed, block, x_ref, a_ref, wt_ref, ut_ref, o_ref, a_all, h, hb, a_sem):
    layers = wt_ref.shape[0]
    n_vars, cols = h.shape
    blocks = cols // block

    def fetch(i):
        rows = pl.ds(pl.multiple_of(i * block, block), block)
        return pltpu.make_async_copy(a_ref.at[rows, :], a_all.at[rows, :], a_sem.at[i])

    @pl.loop(0, blocks)
    def _(i):
        fetch(i).start()

    if packed:
        unpack_kernel(rem, n_vars, x_ref, h, hb.at[0])
    else:
        @pl.loop(0, blocks)
        def _(i):
            here = pl.ds(pl.multiple_of(i * block, block), block)
            h[:, here] = x_ref[:, here]
            hb[0, :, here] = x_ref[:, here].astype(jnp.bfloat16)

    for n in range(layers):
        now, later = n % 2, (n + 1) % 2

        def mix(i):
            if n == 0:
                fetch(i).wait()
            rows = a_all[pl.ds(pl.multiple_of(i * block, block), block), :]
            return lax.dot_general(hb[now], rows, (((1,), (1,)), ((), ())), preferred_element_type=jnp.float32).astype(jnp.bfloat16)

        def update(i, mixed):
            here = pl.ds(pl.multiple_of(i * block, block), block)
            half = jnp.dot(wt_ref[n], mixed, preferred_element_type=jnp.float32)
            arg = half * (2 * GELU_C + (8 * GELU_C * 0.044715) * (half * half))
            act = half * jnp.tanh(arg) + half
            new = h[:, here] + jnp.dot(ut_ref[n], act.astype(jnp.bfloat16), preferred_element_type=jnp.float32)
            h[:, here] = new
            hb[later, :, here] = new.astype(jnp.bfloat16)

        def body(i, mixed):
            following = mix(i)
            update(i - 1, mixed)
            return following

        update(blocks - 1, lax.fori_loop(1, blocks, body, mix(0)))
    pack_kernel(rem, h, o_ref)


def forecast(x, mix_op, wt, ut, n_blocks, block=BLOCK):
    cols = mix_op.shape[0]
    layers, n_vars, hidden = ut.shape
    rem = cols // n_blocks - LANES
    return pl.pallas_call(
        functools.partial(forecast_kernel, rem, x.ndim == 3, block),
        out_shape=jax.ShapeDtypeStruct((n_blocks, n_vars + n_vars * rem // LANES, LANES), jnp.float32),
        in_specs=[VMEM, pl.BlockSpec(memory_space=pl.ANY), VMEM, VMEM],
        out_specs=VMEM,
        scratch_shapes=[
            pltpu.VMEM(mix_op.shape, mix_op.dtype),
            pltpu.VMEM((n_vars, cols), jnp.float32),
            pltpu.VMEM((2, n_vars, cols), jnp.bfloat16),
            pltpu.SemaphoreType.DMA((cols // block,)),
        ],
        compiler_params=pltpu.CompilerParams(vmem_limit_bytes=VMEM_LIMIT),
        cost_estimate=pl.CostEstimate(flops=2 * layers * n_vars * cols * (cols + 2 * hidden), bytes_accessed=2 * cols * cols, transcendentals=layers * hidden * cols),
        name='forecast',
    )(x, mix_op, wt, ut)


def analysis_kernel(n_model, by_output, idx_ref, rho_ref, x_ref, y_ref, r_ref, o_ref, main, rest, pair, out_main, out_rest):
    xa, mean, yo, gy, vec, mats = main
    rxa, rmean, ryo, rgy, rvec, pieces = rest
    t_all, n_all = pair
    n_vars, deep = mean.shape[0], rmean.shape[0]
    n_obs = y_ref.shape[1]
    fold = n_vars // deep
    rem = LANES // fold
    depth = n_vars + deep
    members = x_ref.shape[0] // depth
    groups = members // SUB
    eight = lax.broadcasted_iota(jnp.int32, (SUB, LANES), 0)
    lane_group = lambda rows: lax.broadcasted_iota(jnp.int32, (rows, LANES), 1) // rem
    own_row = lax.broadcasted_iota(jnp.int32, (members, LANES), 0) - SUB * lane_group(members)
    total_eye = (members - 1) / rho_ref[0]

    def spread(x):
        shift = rem
        while shift < LANES:
            x = x + pltpu.roll(x, shift, 1)
            shift *= 2
        return x

    def turns(x):
        return [x] + [pltpu.roll(x, rem * g, 1) for g in range(1, fold)]

    def copies(turned, q):
        away = lax.rem(lane_group(turned[0].shape[0]) + (fold - q), fold)
        out = turned[0]
        for g in range(1, fold):
            out = jnp.where(away == g, turned[g], out)
        return out

    for first, rows, center, mean_ref in ((0, n_vars, xa, mean), (n_vars, deep, rxa, rmean)):
        total = x_ref[first:first + rows, :]
        for k in range(1, members):
            total = total + x_ref[k * depth + first:k * depth + first + rows, :]
        mean_ref[...] = total * (1.0 / members)

        @pl.loop(0, rows // 4)
        def _(v4):
            for c in range(4):
                v = v4 * 4 + c
                center[pl.ds(pl.multiple_of(v * members, SUB), members), :] = x_ref[pl.ds(v + first, members, stride=depth), :] - mean_ref[pl.ds(v, 1), :]

    @pl.loop(0, n_obs // 4)
    def _(p4):
        for c in range(4):
            p = p4 * 4 + c
            var = idx_ref[p]
            row = pl.multiple_of(p * members, SUB)
            here = xa[pl.ds(pl.multiple_of(var * members, SUB), members), :]
            yo[pl.ds(row, members), :] = here
            gy[pl.ds(row, members), :] = here * r_ref[0, pl.ds(p, 1), :]
            vec[pl.ds(p, 1), :] = y_ref[0, pl.ds(p, 1), :] - mean[pl.ds(var, 1), :]
            q, v = var // deep, lax.rem(var, deep)
            here = copies(turns(rxa[pl.ds(pl.multiple_of(v * members, SUB), members), :]), q)
            ryo[pl.ds(row, members), :] = here
            rgy[pl.ds(row, members), :] = here * r_ref[1, pl.ds(p, 1), :]
            level = copies(turns(jnp.broadcast_to(rmean[pl.ds(v, 1), :], (SUB, LANES))), q)
            rvec[pl.ds(p, 1), :] = y_ref[1, pl.ds(p, 1), :] - level[0:1]

    def product(left, left_at, right, right_at, out, out_at, scale=None, diag=None, mirror=True):
        plain = left is gy
        left_row = lambda k, i, a: k * members + SUB * i + a if plain or k < SUB * (i + 1) else (SUB * i + a) * members + k
        for blocks in PASSES:
            def body(kk, acc):
                acc = list(acc)
                for c in range(members):
                    row = c * members
                    for n, i in enumerate(blocks):
                        r = right[pl.ds(pl.multiple_of(right_at + row + SUB * i, SUB), members - SUB * i), :]
                        for a in range(SUB):
                            acc[n * SUB + a] = acc[n * SUB + a] + left[pl.ds(left_at + left_row(c, i, a), 1), :] * r
                return tuple(acc)

            start = [jnp.zeros((members - SUB * i, LANES), jnp.float32) for i in blocks for a in range(SUB)]
            acc = lax.fori_loop(0, 1, body, tuple(start))
            for n, i in enumerate(blocks):
                for a in range(SUB):
                    val = acc[n * SUB + a]
                    val = val if scale is None else val * scale
                    first = val[0:SUB] if diag is None else val[0:SUB] + jnp.where(eight == a, diag, 0.0)
                    row = (SUB * i + a) * members + SUB * i
                    out[pl.ds(pl.multiple_of(out_at + row, SUB), SUB), :] = first
                    if i + 1 < groups:
                        out[pl.ds(pl.multiple_of(out_at + row + SUB, SUB), members - SUB * (i + 1)), :] = val[SUB:]
                        if mirror:
                            out[pl.ds(out_at + SUB * (i + 1) * members + SUB * i + a, members - SUB * (i + 1), stride=members), :] = val[SUB:]


    def split_product(left, left_at, at, depth_k, right, out, out_at, scale=None, diag=None):
        def body(k8, acc):
            for c in range(8):
                k = k8 * 8 + c
                r = right[pl.ds(pl.multiple_of(k * members, SUB), members), :]
                acc = tuple(acc[a] + left[pl.ds(left_at + at(k, a), 1), :] * r for a in range(SUB))
            return acc

        acc = lax.fori_loop(0, depth_k // 8, body, tuple(jnp.zeros((members, LANES), jnp.float32) for a in range(SUB)))
        for a in range(SUB):
            val = acc[a] if scale is None else acc[a] * scale
            out[pl.ds(pl.multiple_of(out_at + a * members, SUB), members), :] = val if diag is None else val + jnp.where(own_row == a, diag, 0.0)

    def copy_all(split, split_at, out):
        @pl.loop(0, SUB // 2)
        def _(a2):
            for c in range(2):
                a = a2 * 2 + c
                turned = turns(split[pl.ds(pl.multiple_of(split_at + a * members, SUB), members), :])
                for q in range(fold):
                    out[pl.ds(pl.multiple_of((SUB * q + a) * members, SUB), members), :] = copies(turned, q)

    by_row = lambda k, a: a * members + k
    square, part = members * members, SUB * members
    slot = lambda n: lax.rem(n + 4 * NS_STEPS, 4)
    whole = lambda n: pl.multiple_of(slot(n) * square, SUB)
    piece = lambda n: pl.multiple_of(slot(n) * part, SUB)

    product(gy, 0, yo, 0, mats, 3 * square, None, total_eye)
    trace = jnp.sum(mats[pl.ds(3 * square, members, stride=members + 1), :], axis=0, keepdims=True)
    inv = 1.0 / trace

    @pl.loop(0, members)
    def _(i):
        row = pl.multiple_of(i * members, SUB)
        bi = mats[pl.ds(3 * square + row, members), :] * inv
        ti = jnp.where(lax.broadcasted_iota(jnp.int32, (members, LANES), 0) == i, 1.5, 0.0) - 0.5 * bi
        mats[pl.ds(row, members), :] = bi
        mats[pl.ds(square + row, members), :] = ti
        mats[pl.ds(2 * square + row, members), :] = ti

    @pl.loop(0, n_obs)
    def _(p):
        x = rgy[pl.ds(pl.multiple_of(p * members, SUB), members), :]
        half = x[0:SUB]
        for q in range(1, fold):
            half = jnp.where(lane_group(SUB) == q, x[SUB * q:SUB * (q + 1)], half)
        n_all[pl.ds(pl.multiple_of(p * SUB, SUB), SUB), :] = half

    split_product(n_all, 0, lambda k, a: k * SUB + a, n_obs, ryo, pieces, 3 * part, None, total_eye)
    rtrace = jnp.zeros((members, LANES), jnp.float32)
    for a in range(SUB):
        rtrace = rtrace + jnp.where(own_row == a, pieces[3 * part + a * members:3 * part + (a + 1) * members, :], 0.0)
    rtrace = spread(jnp.broadcast_to(jnp.sum(rtrace, axis=0, keepdims=True), (SUB, LANES)))[0:1]
    rinv = 1.0 / rtrace
    for a in range(SUB):
        here = slice(a * members, (a + 1) * members)
        bi = pieces[3 * part + a * members:3 * part + (a + 1) * members, :] * rinv
        ti = jnp.where(own_row == a, 1.5, 0.0) - 0.5 * bi
        pieces[a * members:(a + 1) * members, :] = bi
        pieces[part + a * members:part + (a + 1) * members, :] = ti
        pieces[2 * part + a * members:2 * part + (a + 1) * members, :] = ti
    copy_all(pieces, part, t_all)

    @pl.loop(0, NS_STEPS - 1)
    def _(s):
        b, t, z, n = whole(-s), whole(1 - s), whole(2 - s), whole(3 - s)
        rb, rt, rz, rn = piece(-s), piece(1 - s), piece(2 - s), piece(3 - s)
        product(mats, b, mats, t, mats, n)
        split_product(pieces, rb, by_row, members, t_all, pieces, rn)
        copy_all(pieces, rn, n_all)
        product(mats, z, mats, n, mats, b, -0.5, 1.5)
        split_product(pieces, rz, by_row, members, n_all, pieces, rb, -0.5, 1.5)
        copy_all(pieces, rb, t_all)
        product(mats, z, mats, b, mats, t, mirror=False)
        split_product(pieces, rz, by_row, members, t_all, pieces, rt)

    last = 3 - NS_STEPS
    for i in range(groups - 1):
        for a in range(SUB):
            val = mats[pl.ds(whole(last) + (SUB * i + a) * members + SUB * (i + 1), members - SUB * (i + 1)), :]
            mats[pl.ds(whole(last) + SUB * (i + 1) * members + SUB * i + a, members - SUB * (i + 1), stride=members), :] = val
    copy_all(pieces, piece(last), n_all)

    def finish(zs, at, trace, gy, vec, mean, xa, put):
        root = 1.0 / jnp.sqrt(trace)

        def weighted(left, left_at, base, count):
            acc = jnp.zeros((members, LANES), jnp.float32)
            for p in range(count):
                acc = acc + left[pl.ds(left_at + p * members, members), :] * vec[base + p:base + p + 1, :]
            return acc

        vec[n_obs:n_obs + members, :] = weighted(gy, 0, 0, n_obs)
        vec[n_obs + members:n_obs + 2 * members, :] = weighted(zs, at, n_obs, members) * root
        vec[n_obs:n_obs + members, :] = weighted(zs, at, n_obs + members, members) * root

        @pl.loop(0, members)
        def _(i):
            row = pl.multiple_of(i * members, SUB)
            gy[pl.ds(row, members), :] = zs[pl.ds(at + row, members), :] * (root * (members - 1) ** 0.5) + vec[pl.ds(n_obs + i, 1), :]

        @pl.loop(0, mean.shape[0] // 4)
        def _(v4):
            acc = [jnp.broadcast_to(mean[pl.ds(v4 * 4 + c, 1), :], (members, LANES)) for c in range(4)]
            for i in range(members):
                wa = gy[i * members:(i + 1) * members, :]
                acc = [acc[c] + xa[pl.ds((v4 * 4 + c) * members + i, 1), :] * wa for c in range(4)]
            for c in range(4):
                put(v4 * 4 + c, acc[c])

    if not by_output:
        def put(first):
            def store(v, val):
                o_ref[pl.ds(v + first, members, stride=depth), :] = val
            return store

        finish(mats, whole(last), trace, gy, vec, mean, xa, put(0))
        finish(n_all, 0, rtrace, rgy, rvec, rmean, rxa, put(n_vars))
        return

    def put(ref, rows):
        def store(v, val):
            ref[pl.ds(v, members, stride=rows), :] = val
        return store

    finish(mats, whole(last), trace, gy, vec, mean, xa, put(out_main, n_vars))
    finish(n_all, 0, rtrace, rgy, rvec, rmean, rxa, put(out_rest, deep))

    @pl.loop(0, members // n_model)
    def _(e):
        for m in range(n_model):
            row = (e * n_model + m) * depth
            for i in range(n_model):
                k = e * n_model + i
                o_ref[pl.ds(pl.multiple_of(row + deep * i, SUB), deep), :] = out_main[pl.ds(pl.multiple_of(k * n_vars + m * deep, SUB), deep), :]
                x = out_rest[pl.ds(pl.multiple_of(k * deep, SUB), deep), :]
                x = x if i == m else pltpu.roll(x, (rem * (i - m)) % LANES, 1)
                tail = x if i == 0 else jnp.where(lane_group(deep) == i, x, tail)
            o_ref[pl.ds(pl.multiple_of(row + n_vars, SUB), deep), :] = tail


def analysis(x, y, r, obs_idx, inflation, n_vars, n_model, by_output):
    members, depth, _ = x.shape
    n_obs = y.shape[1]
    deep = depth - n_vars
    rows = lambda n: pltpu.VMEM((n, LANES), jnp.float32)
    square, split = members * members, SUB * members
    both = [rows(n_obs * members), rows(n_obs * members), rows(n_obs + 2 * members)]
    return pl.pallas_call(
        functools.partial(analysis_kernel, n_model, by_output),
        out_shape=jax.ShapeDtypeStruct((members * depth, LANES), jnp.float32),
        in_specs=[SMEM, SMEM, VMEM, VMEM, VMEM],
        out_specs=VMEM,
        scratch_shapes=[
            [rows(n_vars * members), rows(n_vars)] + both + [rows(4 * square)],
            [rows(deep * members), rows(deep)] + both + [rows(4 * split)],
            [rows(square), rows(square)],
            rows(members * n_vars if by_output else SUB),
            rows(members * deep if by_output else SUB),
        ],
        name='analysis',
    )(obs_idx, inflation, x.reshape(members * depth, LANES), y, r).reshape(x.shape)


def by_lanes(x):
    x = jnp.swapaxes(x, -1, -2)
    rest = x[..., LANES:]
    rest = jnp.concatenate([rest] * (LANES // rest.shape[-1]), axis=-1)
    return jnp.stack([x[..., :LANES], rest], axis=-3)


def solution(mesh):
    n_model, n_ens = mesh.shape['model'], mesh.shape['ens']

    def local_step(ens_local, mix_op, w_in, w_out, obs_val, obs_prec, obs_idx, inflation):
        held, cols, own_vars = ens_local.shape
        n_blocks = n_model * n_ens
        cycles, layers, n_vars = obs_val.shape[0], w_in.shape[0], w_in.shape[1]
        x = jnp.swapaxes(ens_local, 1, 2)
        h, w_all, u_all = gather_vars(x, w_in, jnp.swapaxes(w_out, 1, 2), n_model)
        h = h.reshape(n_vars, cols)
        wt = (jnp.transpose(w_all, (1, 0, 3, 2)) * jnp.bfloat16(0.5)).reshape(layers, -1, n_vars)
        ut = jnp.transpose(u_all, (1, 2, 0, 3)).reshape(layers, n_vars, -1)
        y = by_lanes(obs_val)
        r = by_lanes(obs_prec)
        x = h
        for cycle in range(cycles):
            last = cycle + 1 == cycles
            x = exchange(forecast(x, mix_op, wt, ut, n_blocks), n_model, n_ens)
            x = analysis(x, y[cycle], r, obs_idx, inflation, n_vars, n_model, last)
            x = exchange(x, n_model, n_ens)
        (h,) = unpack(x, n_vars, (jnp.float32,))
        return jnp.swapaxes(h.reshape(held, own_vars, cols), 1, 2)

    member_spec = P(('case', 'ens'), None, 'model')
    col_axes = ('case', 'ens', 'model')
    in_specs = (member_spec, P(None, None), P(None, None, 'model'), P(None, 'model', None), P(None, col_axes, None), P(col_axes, None), P(None), P(None))
    return jax.shard_map(local_step, mesh=mesh, in_specs=in_specs, out_specs=member_spec, check_vma=False)
```

time: 574 us -> 407 us (0.71)
  Pallas kernels: 560 us -> 398 us
    pallas_call x10 -> x4, Pallas kernels: 421 us -> 262 us  [the longest x2 149 us: forecast(): pl.pallas_call(functools.partial(forecast_kernel, rem, x.ndim == 3, block...]
where the time goes in v2:
time: 407 us; the launch traced here: 406 us
  Pallas kernels  398 us (98%)
    pallas_call x2, Pallas kernels, forecast(): pl.pallas_call(functools.partial(forecast_kernel, rem, x.ndim == 3, block...  149 us
    pallas_call x2, Pallas kernels, analysis(): pl.pallas_call(functools.partial(analysis_kernel, n_model, by_output), ou...  113 us
    pallas_call x4, Pallas kernels, exchange(): pl.pallas_call(functools.partial(exchange_kernel, n_model, n_ens), out_sh...  101 us
    pallas_call x1, Pallas kernels, gather_vars(): pl.pallas_call(functools.partial(gather_vars_kernel, n_model), out_shape=...  31.9 us

profile of v2, /device:TPU:97, one launch (start us, length us, event | category | flops | bytes accessed | tf_op | source)
XLA Modules:
  0.0 405.9 jit_solution(16236824796652342081)
XLA Ops:
  0.7 0.7 slice.29
  1.4 0.8 slice_bitcast_fusion.1
  2.2 0.6 pad_maximum_fusion.1.r_ref
  2.8 0.8 slice.25
  3.6 0.8 slice_bitcast_fusion
  4.4 0.6 fusion.2
  5.0 31.9 %gather_vars.1 = (f32[4,16,5120]{2,1,0:T(8,128)}, bf16[4,3,64,256]{3,2,1,0:T(8,128)(2,1)}, bf16[4,3,64,256]{3,2,1,0:T(8,128)(2,1)}) custom-call(f32[4,16,5120]{2,1,0:T(8,128)} %bitcast.41, bf16[3,64,256]{2,1,0:T(8,128)(2,1)} %w_ref.1, bf16[3,64,256]{2,1,0:T(8,128)(2,1)} %bitcast.43), custom_call_target="tpu_custom_call" | custom-call | tf_op jit(solution)/shard_map/gather_vars/pallas_call | solution.py:48
  37.0 0.0 copy-start
  37.0 1.1 multiply_bitcast_fusion
  38.1 1.2 copy.9
  39.2 0.0 copy-done
  39.2 0.8 copy.12
  40.0 74.3 %forecast.2.x_ref = f32[32,80,128]{2,1,0:T(8,128)} custom-call(f32[64,5120]{1,0:T(8,128)} %bitcast.40, bf16[5120,5120]{1,0:T(8,128)(2,1)} %a_ref.3, bf16[3,1024,64]{2,1,0:T(8,128)(2,1)} %bitcast.32, bf16[3,64,1024]{2,1,0:T(8,128)(2,1)} %bitcast.38), custom_call_target="tpu_custom_call" | custom-call | flops 14092861440 | bytes 52428800 | tf_op jit(solution)/shard_map/forecast/pallas_call | solution.py:207
  114.3 26.7 %exchange.4 = f32[32,80,128]{2,1,0:T(8,128)} custom-call(f32[32,80,128]{2,1,0:T(8,128)} %forecast.2.x_ref), custom_call_target="tpu_custom_call" | custom-call | tf_op jit(solution)/shard_map/exchange/pallas_call | solution.py:79
  141.1 56.1 %analysis.2 = f32[2560,128]{1,0:T(8,128)} custom-call(s32[32]{0:T(128)} %idx_ref.3, f32[1]{0:T(128)S(6)} %copy.13.rho_ref, f32[2560,128]{1,0:T(8,128)} %bitcast.36, f32[2,32,128]{2,1,0:T(8,128)} %get-tuple-element.12.y_ref, f32[2,32,128]{2,1,0:T(8,128)} %pad_maximum_fusion.1.r_ref), custom_call_target="tpu_custom_call" | custom-call | tf_op jit(solution)/shard_map/analysis/pallas_call | solution.py:464
  197.2 24.7 %exchange.5.x_ref = f32[32,80,128]{2,1,0:T(8,128)} custom-call(f32[32,80,128]{2,1,0:T(8,128)} %bitcast.37), custom_call_target="tpu_custom_call" | custom-call | tf_op jit(solution)/shard_map/exchange/pallas_call | solution.py:79
  221.9 74.3 %forecast.3.x_ref = f32[32,80,128]{2,1,0:T(8,128)} custom-call(f32[32,80,128]{2,1,0:T(8,128)} %exchange.5.x_ref, bf16[5120,5120]{1,0:T(8,128)(2,1)} %a_ref.3, bf16[3,1024,64]{2,1,0:T(8,128)(2,1)} %bitcast.33, bf16[3,64,1024]{2,1,0:T(8,128)(2,1)} %bitcast.39), custom_call_target="tpu_custom_call" | custom-call | flops 14092861440 | bytes 52428800 | tf_op jit(solution)/shard_map/forecast/pallas_call | solution.py:207
  296.2 25.7 %exchange.6 = f32[32,80,128]{2,1,0:T(8,128)} custom-call(f32[32,80,128]{2,1,0:T(8,128)} %forecast.3.x_ref), custom_call_target="tpu_custom_call" | custom-call | tf_op jit(solution)/shard_map/exchange/pallas_call | solution.py:79
  321.8 57.1 %analysis.3 = f32[2560,128]{1,0:T(8,128)} custom-call(s32[32]{0:T(128)} %idx_ref.3, f32[1]{0:T(128)S(6)} %copy.13.rho_ref, f32[2560,128]{1,0:T(8,128)} %bitcast.34, f32[2,32,128]{2,1,0:T(8,128)} %get-tuple-element.11.y_ref, f32[2,32,128]{2,1,0:T(8,128)} %pad_maximum_fusion.1.r_ref), custom_call_target="tpu_custom_call" | custom-call | tf_op jit(solution)/shard_map/analysis/pallas_call | solution.py:464
  378.9 23.7 %exchange.7.x_ref = f32[32,80,128]{2,1,0:T(8,128)} custom-call(f32[32,80,128]{2,1,0:T(8,128)} %bitcast.35), custom_call_target="tpu_custom_call" | custom-call | tf_op jit(solution)/shard_map/exchange/pallas_call | solution.py:79
  402.6 3.3 unpack.1
Async XLA Ops:
  37.0 2.3 copy-start

commit v3 on v2

--- a/solution.py
+++ b/solution.py
@@ -8,14 +8,17 @@
 from jax.sharding import PartitionSpec as P
 
 NS_STEPS = 12
+UNROLL = 16
 PASSES = ((0,), (1,), (2, 3))
 LANES = 128
-BLOCK = 256
+BLOCK = 512
+TALL = (True,)
 VMEM_LIMIT = 66_500_000
 GELU_C = 0.7978845608028654
 SUB = 8
 MESH = pl.DeviceIdType.MESH
 VMEM = pl.BlockSpec(memory_space=pltpu.VMEM)
+HBM = pl.BlockSpec(memory_space=pl.ANY)
 SMEM = pl.BlockSpec(memory_space=pltpu.SMEM)
 
 
@@ -79,8 +82,8 @@
     return pl.pallas_call(
         functools.partial(exchange_kernel, n_model, n_ens),
         out_shape=jax.ShapeDtypeStruct(x.shape, x.dtype),
-        in_specs=[VMEM],
-        out_specs=VMEM,
+        in_specs=[HBM],
+        out_specs=HBM,
         scratch_shapes=[pltpu.SemaphoreType.DMA((n_sem,)), pltpu.SemaphoreType.DMA((n_sem,)), pltpu.SemaphoreType.DMA],
         compiler_params=pltpu.CompilerParams(collective_id=1, has_side_effects=True),
         name='exchange',
@@ -177,26 +180,32 @@
         now, later = n % 2, (n + 1) % 2
 
         def mix(i):
-            if n == 0:
-                fetch(i).wait()
-            rows = a_all[pl.ds(pl.multiple_of(i * block, block), block), :]
-            return lax.dot_general(hb[now], rows, (((1,), (1,)), ((), ())), preferred_element_type=jnp.float32).astype(jnp.bfloat16)
+            out = []
+            for j, tall in enumerate(TALL):
+                if n == 0:
+                    fetch(i * len(TALL) + j).wait()
+                rows = a_all[pl.ds(pl.multiple_of((i * len(TALL) + j) * block, block), block), :]
+                pair = (rows, hb[now]) if tall else (hb[now], rows)
+                out.append(lax.dot_general(*pair, (((1,), (1,)), ((), ())), preferred_element_type=jnp.float32).astype(jnp.bfloat16))
+            return tuple(out)
 
         def update(i, mixed):
-            here = pl.ds(pl.multiple_of(i * block, block), block)
-            half = jnp.dot(wt_ref[n], mixed, preferred_element_type=jnp.float32)
-            arg = half * (2 * GELU_C + (8 * GELU_C * 0.044715) * (half * half))
-            act = half * jnp.tanh(arg) + half
-            new = h[:, here] + jnp.dot(ut_ref[n], act.astype(jnp.bfloat16), preferred_element_type=jnp.float32)
-            h[:, here] = new
-            hb[later, :, here] = new.astype(jnp.bfloat16)
+            for j, tall in enumerate(TALL):
+                here = pl.ds(pl.multiple_of((i * len(TALL) + j) * block, block), block)
+                half = lax.dot_general(wt_ref[n], mixed[j], (((1,), (1 if tall else 0,)), ((), ())), preferred_element_type=jnp.float32)
+                arg = half * (2 * GELU_C + (8 * GELU_C * 0.044715) * (half * half))
+                act = half * jnp.tanh(arg) + half
+                new = h[:, here] + jnp.dot(ut_ref[n], act.astype(jnp.bfloat16), preferred_element_type=jnp.float32)
+                h[:, here] = new
+                hb[later, :, here] = new.astype(jnp.bfloat16)
 
         def body(i, mixed):
             following = mix(i)
             update(i - 1, mixed)
             return following
 
-        update(blocks - 1, lax.fori_loop(1, blocks, body, mix(0)))
+        steps = blocks // len(TALL)
+        update(steps - 1, lax.fori_loop(1, steps, body, mix(0)))
     pack_kernel(rem, h, o_ref)
 
 
@@ -285,20 +294,20 @@
 
     def product(left, left_at, right, right_at, out, out_at, scale=None, diag=None, mirror=True):
         plain = left is gy
-        left_row = lambda k, i, a: k * members + SUB * i + a if plain or k < SUB * (i + 1) else (SUB * i + a) * members + k
+        left_row = lambda k, i, a: k * members + SUB * i + a
         for blocks in PASSES:
             def body(kk, acc):
                 acc = list(acc)
-                for c in range(members):
-                    row = c * members
+                for c in range(UNROLL):
+                    row = (kk * UNROLL + c) * members
                     for n, i in enumerate(blocks):
                         r = right[pl.ds(pl.multiple_of(right_at + row + SUB * i, SUB), members - SUB * i), :]
                         for a in range(SUB):
-                            acc[n * SUB + a] = acc[n * SUB + a] + left[pl.ds(left_at + left_row(c, i, a), 1), :] * r
+                            acc[n * SUB + a] = acc[n * SUB + a] + left[pl.ds(left_at + left_row(kk * UNROLL + c, i, a), 1), :] * r
                 return tuple(acc)
 
             start = [jnp.zeros((members - SUB * i, LANES), jnp.float32) for i in blocks for a in range(SUB)]
-            acc = lax.fori_loop(0, 1, body, tuple(start))
+            acc = lax.fori_loop(0, members // UNROLL, body, tuple(start))
             for n, i in enumerate(blocks):
                 for a in range(SUB):
                     val = acc[n * SUB + a]
@@ -336,22 +345,19 @@
 
     by_row = lambda k, a: a * members + k
     square, part = members * members, SUB * members
-    slot = lambda n: lax.rem(n + 4 * NS_STEPS, 4)
-    whole = lambda n: pl.multiple_of(slot(n) * square, SUB)
-    piece = lambda n: pl.multiple_of(slot(n) * part, SUB)
-
-    product(gy, 0, yo, 0, mats, 3 * square, None, total_eye)
-    trace = jnp.sum(mats[pl.ds(3 * square, members, stride=members + 1), :], axis=0, keepdims=True)
+    at_p, at_s, at_v, at_f, at_b, at_z = range(6)
+
+    product(gy, 0, yo, 0, mats, at_s * square, None, total_eye)
+    trace = jnp.sum(mats[pl.ds(at_s * square, members, stride=members + 1), :], axis=0, keepdims=True)
     inv = 1.0 / trace
 
     @pl.loop(0, members)
     def _(i):
         row = pl.multiple_of(i * members, SUB)
-        bi = mats[pl.ds(3 * square + row, members), :] * inv
-        ti = jnp.where(lax.broadcasted_iota(jnp.int32, (members, LANES), 0) == i, 1.5, 0.0) - 0.5 * bi
-        mats[pl.ds(row, members), :] = bi
-        mats[pl.ds(square + row, members), :] = ti
-        mats[pl.ds(2 * square + row, members), :] = ti
+        bi = mats[pl.ds(at_s * square + row, members), :] * inv
+        mats[pl.ds(at_p * square + row, members), :] = bi
+        mats[pl.ds(at_b * square + row, members), :] = bi
+        mats[pl.ds(at_z * square + row, members), :] = jnp.where(lax.broadcasted_iota(jnp.int32, (members, LANES), 0) == i, 1.0, 0.0)
 
     @pl.loop(0, n_obs)
     def _(p):
@@ -361,40 +367,70 @@
             half = jnp.where(lane_group(SUB) == q, x[SUB * q:SUB * (q + 1)], half)
         n_all[pl.ds(pl.multiple_of(p * SUB, SUB), SUB), :] = half
 
-    split_product(n_all, 0, lambda k, a: k * SUB + a, n_obs, ryo, pieces, 3 * part, None, total_eye)
+    split_product(n_all, 0, lambda k, a: k * SUB + a, n_obs, ryo, pieces, at_s * part, None, total_eye)
     rtrace = jnp.zeros((members, LANES), jnp.float32)
     for a in range(SUB):
-        rtrace = rtrace + jnp.where(own_row == a, pieces[3 * part + a * members:3 * part + (a + 1) * members, :], 0.0)
+        rtrace = rtrace + jnp.where(own_row == a, pieces[at_s * part + a * members:at_s * part + (a + 1) * members, :], 0.0)
     rtrace = spread(jnp.broadcast_to(jnp.sum(rtrace, axis=0, keepdims=True), (SUB, LANES)))[0:1]
     rinv = 1.0 / rtrace
     for a in range(SUB):
-        here = slice(a * members, (a + 1) * members)
-        bi = pieces[3 * part + a * members:3 * part + (a + 1) * members, :] * rinv
-        ti = jnp.where(own_row == a, 1.5, 0.0) - 0.5 * bi
-        pieces[a * members:(a + 1) * members, :] = bi
-        pieces[part + a * members:part + (a + 1) * members, :] = ti
-        pieces[2 * part + a * members:2 * part + (a + 1) * members, :] = ti
-    copy_all(pieces, part, t_all)
-
-    @pl.loop(0, NS_STEPS - 1)
+        row = a * members
+        bi = pieces[at_s * part + row:at_s * part + row + members, :] * rinv
+        pieces[at_p * part + row:at_p * part + row + members, :] = bi
+        pieces[at_b * part + row:at_b * part + row + members, :] = bi
+        pieces[at_z * part + row:at_z * part + row + members, :] = jnp.where(own_row == a, 1.0, 0.0)
+
+    def combine(out, diag, p, x):
+        to, of = out
+
+        @pl.loop(0, members // 4)
+        def _(i4):
+            for c in range(4):
+                i = i4 * 4 + c
+                row = pl.multiple_of(i * members, SUB)
+                eye = jnp.where(lax.broadcasted_iota(jnp.int32, (members, LANES), 0) == i, diag, 0.0)
+                mats[pl.ds(to * square + row, members), :] = eye + p * mats[pl.ds(at_p * square + row, members), :] + x * mats[pl.ds(of * square + row, members), :]
+        for a in range(SUB):
+            row = a * members
+            eye = jnp.where(own_row == a, diag, 0.0)
+            pieces[to * part + row:to * part + row + members, :] = eye + p * pieces[at_p * part + row:at_p * part + row + members, :] + x * pieces[of * part + row:of * part + row + members, :]
+
+    def both(left, right, out, copied, mirror=True):
+        product(mats, left * square, mats, right * square, mats, out * square, mirror=mirror)
+        split_product(pieces, left * part, by_row, members, copied, pieces, out * part)
+
+    def move(of, to):
+        @pl.loop(0, SUB)
+        def _(a):
+            here = members * groups
+            mats[pl.ds(pl.multiple_of(to * square + a * here, SUB), here), :] = mats[pl.ds(pl.multiple_of(of * square + a * here, SUB), here), :]
+            pieces[pl.ds(pl.multiple_of(to * part + a * members, SUB), members), :] = pieces[pl.ds(pl.multiple_of(of * part + a * members, SUB), members), :]
+
+    @pl.loop(0, NS_STEPS // 2)
     def _(s):
-        b, t, z, n = whole(-s), whole(1 - s), whole(2 - s), whole(3 - s)
-        rb, rt, rz, rn = piece(-s), piece(1 - s), piece(2 - s), piece(3 - s)
-        product(mats, b, mats, t, mats, n)
-        split_product(pieces, rb, by_row, members, t_all, pieces, rn)
-        copy_all(pieces, rn, n_all)
-        product(mats, z, mats, n, mats, b, -0.5, 1.5)
-        split_product(pieces, rz, by_row, members, n_all, pieces, rb, -0.5, 1.5)
-        copy_all(pieces, rb, t_all)
-        product(mats, z, mats, b, mats, t, mirror=False)
-        split_product(pieces, rz, by_row, members, t_all, pieces, rt)
-
-    last = 3 - NS_STEPS
+        copy_all(pieces, at_p * part, n_all)
+        both(at_p, at_p, at_s, n_all)
+        combine((at_v, at_s), 27.0, -9.0, 1.0)
+        copy_all(pieces, at_s * part, n_all)
+        both(at_v, at_s, at_f, n_all)
+        combine((at_f, at_f), 36.0 / 16, -39.0 / 16, 1.0 / 16)
+        copy_all(pieces, at_f * part, t_all)
+        both(at_z, at_f, at_s, t_all)
+        move(at_s, at_z)
+
+        @pl.when(s + 1 < NS_STEPS // 2)
+        def _():
+            both(at_b, at_f, at_v, t_all)
+            copy_all(pieces, at_v * part, n_all)
+            both(at_z, at_v, at_p, n_all)
+            move(at_v, at_b)
+
+    z_row = at_z * square
     for i in range(groups - 1):
         for a in range(SUB):
-            val = mats[pl.ds(whole(last) + (SUB * i + a) * members + SUB * (i + 1), members - SUB * (i + 1)), :]
-            mats[pl.ds(whole(last) + SUB * (i + 1) * members + SUB * i + a, members - SUB * (i + 1), stride=members), :] = val
-    copy_all(pieces, piece(last), n_all)
+            val = mats[pl.ds(z_row + (SUB * i + a) * members + SUB * (i + 1), members - SUB * (i + 1)), :]
+            mats[pl.ds(z_row + SUB * (i + 1) * members + SUB * i + a, members - SUB * (i + 1), stride=members), :] = val
+    copy_all(pieces, at_z * part, n_all)
 
     def finish(zs, at, trace, gy, vec, mean, xa, put):
         root = 1.0 / jnp.sqrt(trace)
@@ -429,7 +465,7 @@
                 o_ref[pl.ds(v + first, members, stride=depth), :] = val
             return store
 
-        finish(mats, whole(last), trace, gy, vec, mean, xa, put(0))
+        finish(mats, z_row, trace, gy, vec, mean, xa, put(0))
         finish(n_all, 0, rtrace, rgy, rvec, rmean, rxa, put(n_vars))
         return
 
@@ -438,7 +474,7 @@
             ref[pl.ds(v, members, stride=rows), :] = val
         return store
 
-    finish(mats, whole(last), trace, gy, vec, mean, xa, put(out_main, n_vars))
+    finish(mats, z_row, trace, gy, vec, mean, xa, put(out_main, n_vars))
     finish(n_all, 0, rtrace, rgy, rvec, rmean, rxa, put(out_rest, deep))
 
     @pl.loop(0, members // n_model)
@@ -467,8 +503,8 @@
         in_specs=[SMEM, SMEM, VMEM, VMEM, VMEM],
         out_specs=VMEM,
         scratch_shapes=[
-            [rows(n_vars * members), rows(n_vars)] + both + [rows(4 * square)],
-            [rows(deep * members), rows(deep)] + both + [rows(4 * split)],
+            [rows(n_vars * members), rows(n_vars)] + both + [rows(6 * square)],
+            [rows(deep * members), rows(deep)] + both + [rows(6 * split)],
             [rows(square), rows(square)],
             rows(members * n_vars if by_output else SUB),
             rows(members * deep if by_output else SUB),

time: 407 us -> 380 us (0.934)
  Pallas kernels: 398 us -> 371 us
    pallas_call x2, Pallas kernels: 149 us -> 132 us  [forecast(): pl.pallas_call(functools.partial(forecast_kernel, rem, x.ndim == 3, block...]
    pallas_call x4, Pallas kernels: 101 us -> 90.7 us  [exchange(): pl.pallas_call(functools.partial(exchange_kernel, n_model, n_ens), out_sh...]
where the time goes in v3:
time: 380 us; the launch traced here: 379 us
  Pallas kernels  371 us (98%)
  other arithmetic  3.97 us (1%)
    pallas_call x2, Pallas kernels, forecast(): pl.pallas_call(functools.partial(forecast_kernel, rem, x.ndim == 3, block...  132 us
    pallas_call x2, Pallas kernels, analysis(): pl.pallas_call(functools.partial(analysis_kernel, n_model, by_output), ou...  113 us
    pallas_call x4, Pallas kernels, exchange(): pl.pallas_call(functools.partial(exchange_kernel, n_model, n_ens), out_sh...  90.7 us
    pallas_call x1, Pallas kernels, gather_vars(): pl.pallas_call(functools.partial(gather_vars_kernel, n_model), out_shape=...  31.9 us

profile of v3, /device:TPU:97, one launch (start us, length us, event | category | flops | bytes accessed | tf_op | source)
XLA Modules:
  0.0 379.0 jit_solution(15591446296831776867)
XLA Ops:
  0.7 0.7 slice.29
  1.4 0.8 slice_bitcast_fusion.1
  2.2 0.6 pad_maximum_fusion.1.r_ref
  2.8 0.8 slice.25
  3.6 0.8 slice_bitcast_fusion
  4.4 0.6 fusion.2
  5.0 31.9 %gather_vars.1 = (f32[4,16,5120]{2,1,0:T(8,128)}, bf16[4,3,64,256]{3,2,1,0:T(8,128)(2,1)}, bf16[4,3,64,256]{3,2,1,0:T(8,128)(2,1)}) custom-call(f32[4,16,5120]{2,1,0:T(8,128)} %bitcast.41, bf16[3,64,256]{2,1,0:T(8,128)(2,1)} %w_ref.1, bf16[3,64,256]{2,1,0:T(8,128)(2,1)} %bitcast.43), custom_call_target="tpu_custom_call" | custom-call | tf_op jit(solution)/shard_map/gather_vars/pallas_call | solution.py:51
  37.0 0.0 copy-start
  37.0 1.1 multiply_bitcast_fusion
  38.1 1.2 copy.9
  39.2 0.0 copy-done
  39.2 0.8 copy.12
  40.0 65.9 %forecast.2.x_ref = f32[32,80,128]{2,1,0:T(8,128)} custom-call(f32[64,5120]{1,0:T(8,128)} %bitcast.40, bf16[5120,5120]{1,0:T(8,128)(2,1)} %a_ref.3, bf16[3,1024,64]{2,1,0:T(8,128)(2,1)} %bitcast.32, bf16[3,64,1024]{2,1,0:T(8,128)(2,1)} %bitcast.38), custom_call_target="tpu_custom_call" | custom-call | flops 14092861440 | bytes 52428800 | tf_op jit(solution)/shard_map/forecast/pallas_call | solution.py:216
  106.0 24.7 %exchange.4 = f32[32,80,128]{2,1,0:T(8,128)} custom-call(f32[32,80,128]{2,1,0:T(8,128)} %forecast.2.x_ref), custom_call_target="tpu_custom_call" | custom-call | tf_op jit(solution)/shard_map/exchange/pallas_call | solution.py:82
  130.7 56.0 %analysis.2 = f32[2560,128]{1,0:T(8,128)} custom-call(s32[32]{0:T(128)} %idx_ref.3, f32[1]{0:T(128)S(6)} %copy.13.rho_ref, f32[2560,128]{1,0:T(8,128)} %bitcast.36, f32[2,32,128]{2,1,0:T(8,128)} %get-tuple-element.12.y_ref, f32[2,32,128]{2,1,0:T(8,128)} %pad_maximum_fusion.1.r_ref), custom_call_target="tpu_custom_call" | custom-call | tf_op jit(solution)/shard_map/analysis/pallas_call | solution.py:500
  186.7 21.9 %exchange.5.x_ref = f32[32,80,128]{2,1,0:T(8,128)} custom-call(f32[32,80,128]{2,1,0:T(8,128)} %bitcast.37), custom_call_target="tpu_custom_call" | custom-call | tf_op jit(solution)/shard_map/exchange/pallas_call | solution.py:82
  208.6 66.1 %forecast.3.x_ref = f32[32,80,128]{2,1,0:T(8,128)} custom-call(f32[32,80,128]{2,1,0:T(8,128)} %exchange.5.x_ref, bf16[5120,5120]{1,0:T(8,128)(2,1)} %a_ref.3, bf16[3,1024,64]{2,1,0:T(8,128)(2,1)} %bitcast.33, bf16[3,64,1024]{2,1,0:T(8,128)(2,1)} %bitcast.39), custom_call_target="tpu_custom_call" | custom-call | flops 14092861440 | bytes 52428800 | tf_op jit(solution)/shard_map/forecast/pallas_call | solution.py:216
  274.7 21.6 %exchange.6 = f32[32,80,128]{2,1,0:T(8,128)} custom-call(f32[32,80,128]{2,1,0:T(8,128)} %forecast.3.x_ref), custom_call_target="tpu_custom_call" | custom-call | tf_op jit(solution)/shard_map/exchange/pallas_call | solution.py:82
  296.3 56.8 %analysis.3 = f32[2560,128]{1,0:T(8,128)} custom-call(s32[32]{0:T(128)} %idx_ref.3, f32[1]{0:T(128)S(6)} %copy.13.rho_ref, f32[2560,128]{1,0:T(8,128)} %bitcast.34, f32[2,32,128]{2,1,0:T(8,128)} %get-tuple-element.11.y_ref, f32[2,32,128]{2,1,0:T(8,128)} %pad_maximum_fusion.1.r_ref), custom_call_target="tpu_custom_call" | custom-call | tf_op jit(solution)/shard_map/analysis/pallas_call | solution.py:500
  353.2 22.5 %exchange.7.x_ref = f32[32,80,128]{2,1,0:T(8,128)} custom-call(f32[32,80,128]{2,1,0:T(8,128)} %bitcast.35), custom_call_target="tpu_custom_call" | custom-call | tf_op jit(solution)/shard_map/exchange/pallas_call | solution.py:82
  375.6 3.3 unpack.1
Async XLA Ops:
  37.0 2.3 copy-start

commit v4 on v3

--- a/solution.py
+++ b/solution.py
@@ -29,34 +29,46 @@
     pl.semaphore_wait(barrier, len(peers))
 
 
-def gather_vars_kernel(n_model, x_ref, w_ref, u_ref, h_ref, wa_ref, ua_ref, send_sem, recv_sem, own_sem):
-    me = lax.axis_index('model')
-    others = [lax.rem(me + t, n_model) for t in range(1, n_model)]
-    greet([{'model': o} for o in others])
-    copies = []
-    for t, o in enumerate(others):
-        for a, (src, dst) in enumerate(((x_ref.at[o], h_ref.at[me]), (w_ref, wa_ref.at[me]), (u_ref, ua_ref.at[me]))):
-            copies.append(pltpu.make_async_remote_copy(src_ref=src, dst_ref=dst, send_sem=send_sem.at[3 * t + a], recv_sem=recv_sem.at[3 * t + a], device_id={'model': o}, device_id_type=MESH))
-    for copy in copies:
+def gather_vars_kernel(n_model, n_ens, x_ref, w_ref, h_ref, wa_ref, send_sem, recv_sem, own_sem):
+    me, mine = lax.axis_index('model'), lax.axis_index('ens')
+    tiles = w_ref.shape[0] // n_ens
+    part = pl.ds(mine * tiles, tiles)
+    around = [lax.rem(me + t, n_model) for t in range(1, n_model)]
+    along = [lax.rem(mine + t, n_ens) for t in range(1, n_ens)]
+    greet([{'model': o} for o in around] + [{'ens': o} for o in along])
+    count = iter(range(send_sem.shape[0]))
+
+    def remote(src, dst, where):
+        i = next(count)
+        return pltpu.make_async_remote_copy(src_ref=src, dst_ref=dst, send_sem=send_sem.at[i], recv_sem=recv_sem.at[i], device_id=where, device_id_type=MESH)
+
+    shards = [remote(w_ref.at[part], wa_ref.at[me, part], {'model': o}) for o in around]
+    members = [remote(x_ref.at[o], h_ref.at[me], {'model': o}) for o in around]
+    for copy in shards + members:
         copy.start()
-    own = [pltpu.make_async_copy(src, dst, own_sem.at[a]) for a, (src, dst) in enumerate(((x_ref.at[me], h_ref.at[me]), (w_ref, wa_ref.at[me]), (u_ref, ua_ref.at[me])))]
+    own = [pltpu.make_async_copy(x_ref.at[me], h_ref.at[me], own_sem.at[0]), pltpu.make_async_copy(w_ref, wa_ref.at[me], own_sem.at[1])]
     for copy in own:
         copy.start()
-    for copy in own + copies:
+    for copy in shards:
         copy.wait()
-
-
-def gather_vars(x, w, u, n_model):
-    n_sem = 3 * (n_model - 1)
+    onward = [remote(wa_ref.at[s, part], wa_ref.at[s, part], {'ens': o}) for o in along for s in around]
+    for copy in onward:
+        copy.start()
+    for copy in own + members + onward:
+        copy.wait()
+
+
+def gather_vars(x, w, n_model, n_ens):
+    n_sem = (n_model - 1) * (n_ens + 1)
     return pl.pallas_call(
-        functools.partial(gather_vars_kernel, n_model),
-        out_shape=(jax.ShapeDtypeStruct(x.shape, x.dtype), jax.ShapeDtypeStruct((n_model,) + w.shape, w.dtype), jax.ShapeDtypeStruct((n_model,) + u.shape, u.dtype)),
-        in_specs=[VMEM] * 3,
-        out_specs=[VMEM] * 3,
-        scratch_shapes=[pltpu.SemaphoreType.DMA((n_sem,)), pltpu.SemaphoreType.DMA((n_sem,)), pltpu.SemaphoreType.DMA((3,))],
+        functools.partial(gather_vars_kernel, n_model, n_ens),
+        out_shape=(jax.ShapeDtypeStruct(x.shape, x.dtype), jax.ShapeDtypeStruct((n_model,) + w.shape, w.dtype)),
+        in_specs=[VMEM] * 2,
+        out_specs=[VMEM] * 2,
+        scratch_shapes=[pltpu.SemaphoreType.DMA((n_sem,)), pltpu.SemaphoreType.DMA((n_sem,)), pltpu.SemaphoreType.DMA((2,))],
         compiler_params=pltpu.CompilerParams(collective_id=0, has_side_effects=True),
         name='gather_vars',
-    )(x, w, u)
+    )(x, w)
 
 
 def exchange_kernel(n_model, n_ens, x_ref, o_ref, send_sem, recv_sem, own_sem):
@@ -528,10 +540,12 @@
         n_blocks = n_model * n_ens
         cycles, layers, n_vars = obs_val.shape[0], w_in.shape[0], w_in.shape[1]
         x = jnp.swapaxes(ens_local, 1, 2)
-        h, w_all, u_all = gather_vars(x, w_in, jnp.swapaxes(w_out, 1, 2), n_model)
+        w_own = jnp.concatenate([w_in, jnp.swapaxes(w_out, 1, 2)])
+        h, w_all = gather_vars(x, w_own.reshape(-1, 2 * SUB, w_own.shape[2]), n_model, n_ens)
         h = h.reshape(n_vars, cols)
-        wt = (jnp.transpose(w_all, (1, 0, 3, 2)) * jnp.bfloat16(0.5)).reshape(layers, -1, n_vars)
-        ut = jnp.transpose(u_all, (1, 2, 0, 3)).reshape(layers, n_vars, -1)
+        w_all = w_all.reshape((n_model,) + w_own.shape)
+        wt = (jnp.transpose(w_all[:, :layers], (1, 0, 3, 2)) * jnp.bfloat16(0.5)).reshape(layers, -1, n_vars)
+        ut = jnp.transpose(w_all[:, layers:], (1, 2, 0, 3)).reshape(layers, n_vars, -1)
         y = by_lanes(obs_val)
         r = by_lanes(obs_prec)
         x = h

time: 380 us -> 379 us (level)
    pallas_call x1, Pallas kernels: 31.9 us -> 27.3 us  [gather_vars(): pl.pallas_call(functools.partial(gather_vars_kernel, n_model, n_ens), out...]
where the time goes in v4:
time: 379 us; the launch traced here: 378 us
  Pallas kernels  368 us (97%)
  other arithmetic  5.49 us (1%)
  local copies, waits for them, and re-layouts  4.35 us (1%)
    pallas_call x2, Pallas kernels, forecast(): pl.pallas_call(functools.partial(forecast_kernel, rem, x.ndim == 3, block...  132 us
    pallas_call x2, Pallas kernels, analysis(): pl.pallas_call(functools.partial(analysis_kernel, n_model, by_output), ou...  113 us
    pallas_call x4, Pallas kernels, exchange(): pl.pallas_call(functools.partial(exchange_kernel, n_model, n_ens), out_sh...  92.1 us
    pallas_call x1, Pallas kernels, gather_vars(): pl.pallas_call(functools.partial(gather_vars_kernel, n_model, n_ens), out...  27.3 us

profile of v4, /device:TPU:97, one launch (start us, length us, event | category | flops | bytes accessed | tf_op | source)
XLA Modules:
  0.0 378.2 jit_solution(15270092536764223051)
XLA Ops:
  0.7 0.7 slice.39
  1.4 0.8 slice_bitcast_fusion.1
  2.2 0.6 pad_maximum_fusion.2.r_ref
  2.8 0.8 slice.35
  3.6 0.8 slice_bitcast_fusion
  4.4 0.6 fusion.2
  5.0 1.6 pad_maximum_fusion
  6.7 27.3 %gather_vars.1 = (f32[4,16,5120]{2,1,0:T(8,128)}, bf16[4,24,16,256]{3,2,1,0:T(8,128)(2,1)}) custom-call(f32[4,16,5120]{2,1,0:T(8,128)} %bitcast.42, bf16[24,16,256]{2,1,0:T(8,128)(2,1)} %bitcast.44), custom_call_target="tpu_custom_call" | custom-call | tf_op jit(solution)/shard_map/gather_vars/pallas_call | solution.py:63
  34.0 1.2 fusion.3
  35.2 0.3 copy.15
  35.5 1.0 reshape.34.ut_ref
  36.5 0.4 copy.12
  36.9 1.0 broadcast_multiply_fusion
  37.9 65.9 %forecast.2.x_ref = f32[32,80,128]{2,1,0:T(8,128)} custom-call(f32[64,5120]{1,0:T(8,128)} %bitcast.41, bf16[5120,5120]{1,0:T(8,128)(2,1)} %a_ref.3, bf16[3,1024,64]{2,1,0:T(8,128)(2,1)} %bitcast.34, bf16[3,64,1024]{2,1,0:T(8,128)(2,1)} %reshape.34.ut_ref), custom_call_target="tpu_custom_call" | custom-call | flops 14092861440 | bytes 52428800 | tf_op jit(solution)/shard_map/forecast/pallas_call | solution.py:228
  103.8 24.0 %exchange.4 = f32[32,80,128]{2,1,0:T(8,128)} custom-call(f32[32,80,128]{2,1,0:T(8,128)} %forecast.2.x_ref), custom_call_target="tpu_custom_call" | custom-call | tf_op jit(solution)/shard_map/exchange/pallas_call | solution.py:94
  127.8 56.0 %analysis.2 = f32[2560,128]{1,0:T(8,128)} custom-call(s32[32]{0:T(128)} %idx_ref.3, f32[1]{0:T(128)S(6)} %copy.16.rho_ref, f32[2560,128]{1,0:T(8,128)} %bitcast.38, f32[2,32,128]{2,1,0:T(8,128)} %get-tuple-element.12.y_ref, f32[2,32,128]{2,1,0:T(8,128)} %pad_maximum_fusion.2.r_ref), custom_call_target="tpu_custom_call" | custom-call | tf_op jit(solution)/shard_map/analysis/pallas_call | solution.py:512
  183.8 22.0 %exchange.5.x_ref = f32[32,80,128]{2,1,0:T(8,128)} custom-call(f32[32,80,128]{2,1,0:T(8,128)} %bitcast.39), custom_call_target="tpu_custom_call" | custom-call | tf_op jit(solution)/shard_map/exchange/pallas_call | solution.py:94
  205.8 66.1 %forecast.3.x_ref = f32[32,80,128]{2,1,0:T(8,128)} custom-call(f32[32,80,128]{2,1,0:T(8,128)} %exchange.5.x_ref, bf16[5120,5120]{1,0:T(8,128)(2,1)} %a_ref.3, bf16[3,1024,64]{2,1,0:T(8,128)(2,1)} %bitcast.35, bf16[3,64,1024]{2,1,0:T(8,128)(2,1)} %reshape.34.ut_ref), custom_call_target="tpu_custom_call" | custom-call | flops 14092861440 | bytes 52428800 | tf_op jit(solution)/shard_map/forecast/pallas_call | solution.py:228
  272.0 22.5 %exchange.6 = f32[32,80,128]{2,1,0:T(8,128)} custom-call(f32[32,80,128]{2,1,0:T(8,128)} %forecast.3.x_ref), custom_call_target="tpu_custom_call" | custom-call | tf_op jit(solution)/shard_map/exchange/pallas_call | solution.py:94
  294.4 56.8 %analysis.3 = f32[2560,128]{1,0:T(8,128)} custom-call(s32[32]{0:T(128)} %idx_ref.3, f32[1]{0:T(128)S(6)} %copy.16.rho_ref, f32[2560,128]{1,0:T(8,128)} %bitcast.36, f32[2,32,128]{2,1,0:T(8,128)} %get-tuple-element.11.y_ref, f32[2,32,128]{2,1,0:T(8,128)} %pad_maximum_fusion.2.r_ref), custom_call_target="tpu_custom_call" | custom-call | tf_op jit(solution)/shard_map/analysis/pallas_call | solution.py:512
  351.2 23.6 %exchange.7.x_ref = f32[32,80,128]{2,1,0:T(8,128)} custom-call(f32[32,80,128]{2,1,0:T(8,128)} %bitcast.37), custom_call_target="tpu_custom_call" | custom-call | tf_op jit(solution)/shard_map/exchange/pallas_call | solution.py:94
  374.9 3.3 unpack.1
